TPU v7x, 32 devices: a whole 2x2x4 slice. The times are simulated.
32 devices in a mesh: rows: 16 (over z, x, core), cols: 2 (over y).
Axes of the slice: x: 2, y: 2, z: 4, core: 2. Of those that a mesh axis runs over, the one named last changes fastest.
Arguments:
- kets: float32 [16, 4, 32], P('rows', 'cols'), may hold values from -3 to 3
- left_maps: float32 [2, 16, 4, 96, 384], P(None, 'rows', 'cols'), may hold values from -0.3125 to 0.3125
- right_maps: float32 [2, 16, 4, 96, 384], P(None, 'rows', 'cols'), may hold values from -0.3125 to 0.3125
- top_edge: float32 [4, 96, 384], P('cols'), may hold values from -6 to 6
- bottom_edge: float32 [4, 96, 384], P('cols'), may hold values from -6 to 6
- left_edge: float32 [16, 96, 384], P('rows'), may hold values from -6 to 6
- right_edge: float32 [16, 96, 384], P('rows'), may hold values from -6 to 6
- term_rows: int32 [16], replicated, may hold values from 0 to 15
- term_bonds: int32 [16], replicated, may hold values from 0 to 2
- term_ops: int32 [16], replicated, may hold values from 0 to 3
- operators: float32 [4, 16], replicated, may hold values from -6 to 6
Outputs:
- top_out: float32 [16, 4, 96, 384], P('rows', 'cols')
- bottom_out: float32 [16, 4, 96, 384], P('rows', 'cols')
- energies: float32 [16], replicated
Inputs may be any that keep to these rules, and one draw needn't show every extreme that they name: Term t acts on the bond between columns term_bonds[t] and term_bonds[t] + 1 of row term_rows[t].
All inputs are finite; a program needn't handle non-finite values.
Results may differ from a plain program's by a relative error of at most 0.0003.
Values sent between devices are 32-bit elements; how exact they have to be, the bound alone decides.
A program may use at most 64 MiB of HBM per device.

v0:
```python
import functools

import jax
import jax.numpy as jnp
from jax import lax
from jax.experimental import pallas as pl
from jax.experimental.pallas import tpu as pltpu
from jax.sharding import PartitionSpec as P

D = 2
D2 = 4
PHYS = 2
EPSILON = 1e-06
LANES = 128


def unpack_lanes(tiles, chi):
    rolled = {}
    lane = lax.broadcasted_iota(jnp.int32, tiles[0].shape, 1)
    blocks = []
    for block in range(D2):
        total = jnp.zeros_like(tiles[0])
        for place, tile in enumerate(tiles):
            low = max(chi * block, LANES * place)
            high = min(chi * (block + 1), LANES * (place + 1))
            if low >= high:
                continue
            shift = (LANES * place - chi * block) % LANES
            if (place, shift) not in rolled:
                rolled[place, shift] = tile if shift == 0 else pltpu.roll(tile, shift, 1)
            inside = (lane >= low - chi * block) & (lane < high - chi * block)
            total = jnp.where(inside, rolled[place, shift], total)
        blocks.append(total)
    return blocks


def pack_lanes(blocks, chi):
    lane = lax.broadcasted_iota(jnp.int32, blocks[0].shape, 1)
    rolled = {}
    tiles = []
    for place in range(chi * D2 // LANES):
        total = jnp.zeros_like(blocks[0])
        for block, values in enumerate(blocks):
            low = max(chi * block, LANES * place)
            high = min(chi * (block + 1), LANES * (place + 1))
            if low >= high:
                continue
            shift = (chi * block - LANES * place) % LANES
            if (block, shift) not in rolled:
                rolled[block, shift] = values if shift == 0 else pltpu.roll(values, shift, 1)
            inside = (lane >= low - LANES * place) & (lane < high - LANES * place)
            total = jnp.where(inside, rolled[block, shift], total)
        tiles.append(total)
    return tiles


def halves(values):
    high = values.astype(jnp.bfloat16)
    low = (values - high.astype(jnp.float32)).astype(jnp.bfloat16)
    return high, low


def dot32(former, latter):
    return jnp.dot(former, latter, preferred_element_type=jnp.float32)


def dot_last(former, latter):
    return lax.dot_general(
        former, latter, (((1,), (1,)), ((), ())), preferred_element_type=jnp.float32
    )


def load_tiles(ref, at, width):
    return [ref[at, :, LANES * t : LANES * (t + 1)] for t in range(width // LANES)]


def window_kernel(
    row_count,
    col_count,
    kets_ref,
    left_maps_ref,
    right_maps_ref,
    top_ref,
    bottom_ref,
    left_ref,
    right_ref,
    rows_ref,
    bonds_ref,
    ops_ref,
    table_ref,
    out_ref,
    energy_ref,
    kets,
    kets_env,
    maps,
    edges,
    sides,
    env_ref,
    pbuf,
    qbuf,
    kbuf,
    xbuf,
    ebuf,
    pick,
    pboth,
    qhi,
    qlo,
    x32,
    jbuf,
    thi,
    tlo,
    near,
    far,
    vbuf,
    opens,
    hop_out,
    hop_in,
    half_out,
    half_in,
    shares,
    row_share,
    load_sem,
    map_send,
    map_recv,
    env_send,
    env_recv,
    out_send,
    out_recv,
    chain_send,
    chain_recv,
    hop_send,
    hop_recv,
    half_send,
    half_recv,
    share_send,
    share_recv,
):
    local_cols = kets.shape[1]
    chi, width = maps.shape[3], maps.shape[4]
    half = chi // 2
    wide = D2 * LANES
    pairs = PHYS * PHYS
    terms = rows_ref.shape[1]
    tall = shares.shape[1:]
    group = 2 * local_cols
    groups = row_count // group
    place = lax.axis_index("rows")
    cols_at = lax.axis_index("cols")
    has_left = cols_at > 0
    has_right = cols_at < col_count - 1
    mine = place // group
    me = place % group
    column = me // 2
    way = me % 2
    base = mine * group
    before = mine - 1 + 2 * way
    after = mine + 1 - 2 * way
    has_before = (before >= 0) & (before < groups)
    has_after = (after >= 0) & (after < groups)

    barrier = pltpu.get_barrier_semaphore()
    for other in range(row_count):

        @pl.when(place != other)
        def _():
            pl.semaphore_signal(barrier, inc=1, device_id={"rows": other})

    for other in range(col_count):

        @pl.when(cols_at != other)
        def _():
            pl.semaphore_signal(barrier, inc=1, device_id={"cols": other})

    loads = [
        pltpu.make_async_copy(source, target, load_sem.at[at])
        for at, (source, target) in enumerate(
            (
                (right_maps_ref.at[:, 0], maps.at[0]),
                (left_maps_ref.at[:, 0], maps.at[1]),
                (top_ref, edges.at[0]),
                (bottom_ref, edges.at[1]),
                (left_ref, sides.at[pl.ds(0, 1)]),
                (right_ref, sides.at[pl.ds(1, 1)]),
            )
        )
    ]
    for load in loads:
        load.start()

    count = kets_ref.shape[2]
    spot = lax.broadcasted_iota(jnp.int32, (count, count), 0)
    from_lane = lax.broadcasted_iota(jnp.int32, (count, count), 1)

    def exchanged(high, low):
        top, bottom = (spot // high) % 2, (spot // low) % 2
        return spot + (bottom - top) * high + (top - bottom) * low

    for order, target in ((spot, 0), (exchanged(8, 2), 1), (exchanged(4, 1), 2)):
        for at in range(local_cols):
            values = jnp.broadcast_to(kets_ref[0, at : at + 1, :], (count, count))
            tallest = jnp.sum(
                jnp.where(order == from_lane, values, 0.0), axis=1, keepdims=True
            )
            filled = jnp.broadcast_to(tallest, (count, LANES))
            if target < 2:
                kets[target, at] = filled
            if target != 1:
                kets_env[target // 2, at] = filled

    chosen = lax.broadcasted_iota(jnp.int32, (wide, width), 0)
    entry = lax.broadcasted_iota(jnp.int32, (wide, width), 1)
    wanted = (chosen % LANES) * D2 + chosen // LANES
    live = (chosen % LANES) < chi
    pick[...] = jnp.where((wanted == entry) & live, 1.0, 0.0).astype(jnp.bfloat16)
    thi[...] = jnp.zeros_like(thi)
    tlo[...] = jnp.zeros_like(tlo)
    for load in loads:
        load.wait()
    pl.semaphore_wait(barrier, row_count - 1 + col_count - 1)

    def map_copies(target_way, target_col, target, local):
        made = []
        for kind, (source, buffer) in enumerate(
            ((kets, kbuf), (maps.at[0], qbuf), (maps.at[1], pbuf))
        ):
            origin, landing = source.at[target_way, target_col], buffer.at[me]
            if local:
                made.append(pltpu.make_async_copy(origin, landing, map_recv.at[kind, me]))
            else:
                made.append(
                    pltpu.make_async_remote_copy(
                        origin,
                        landing,
                        map_send.at[kind, target],
                        map_recv.at[kind, me],
                        device_id={"rows": base + target},
                    )
                )
        return made

    low_half = jnp.where(mine >= groups // 2, 1, 0)
    for turn in range(group):
        target_way = (low_half + turn // local_cols) % 2
        target_col = turn % local_cols
        target = target_col * 2 + target_way

        @pl.when(target != me)
        def _():
            for copy in map_copies(target_way, target_col, target, False):
                copy.start()

        @pl.when(target == me)
        def _():
            for copy in map_copies(target_way, target_col, target, True):
                copy.start()

    def prepare(step, unused):
        slot = step + way * (group - 1 - 2 * step)
        for kind, buffer in enumerate((kbuf, qbuf, pbuf)):
            pltpu.make_async_copy(
                buffer.at[slot], buffer.at[slot], map_recv.at[kind, slot]
            ).wait()
        ket = kbuf[slot]
        half = ket.shape[0] // PHYS
        for i in range(half):
            total = ket[i : i + 1] * ket[0:half]
            for p in range(1, PHYS):
                total += ket[p * half + i : p * half + i + 1] * ket[p * half : (p + 1) * half]
            ebuf[step, i * half : (i + 1) * half] = total
        values = pick[...]
        for source, high_ref, low_ref, right in (
            (qbuf, qhi, qlo, True),
            (pbuf, pboth, pboth, False),
        ):
            for at, (part, ref) in enumerate(zip(halves(source[slot]), (high_ref, low_ref))):
                if right:
                    fill = jnp.zeros((LANES - chi, width), jnp.bfloat16)
                    tall = dot_last(values, jnp.concatenate([part, fill], axis=0))
                    for w in range(D2):
                        ref[step, :, w * LANES : (w + 1) * LANES] = tall[
                            w * LANES : (w + 1) * LANES
                        ].astype(jnp.bfloat16)
                else:
                    spread_map = dot_last(part, values).astype(jnp.bfloat16)
                    ref[step, at * chi : (at + 1) * chi] = spread_map
        return unused

    def row_copy(source, landing, send, recv, slot):
        remote = pltpu.make_async_remote_copy(
            source, landing, send, recv, device_id={"rows": base + slot}
        )
        return remote, pltpu.make_async_copy(source, landing, recv)

    def send_row(source, landing, send, recv, slot):
        remote, local = row_copy(source, landing, send, recv, slot)

        @pl.when(slot != me)
        def _():
            remote.start()

        @pl.when(slot == me)
        def _():
            local.start()

    chain_hop = pltpu.make_async_remote_copy(
        xbuf.at[group],
        xbuf.at[0],
        chain_send,
        chain_recv,
        device_id={"rows": after * group + me},
    )

    start_slot = way * (group - 1)
    crossing = jnp.logical_not(has_before) & ((start_slot // local_cols) != (me // local_cols))
    ahead = jnp.where(has_before, group, jnp.where(crossing, group - local_cols + 1, 1))
    turned_by = jnp.where(crossing, local_cols, 0)

    def prepare_ahead(turn, unused):
        return prepare((turn + turned_by) % group, unused)

    lax.fori_loop(0, ahead, prepare_ahead, 0)

    @pl.when(has_before)
    def _():
        pltpu.make_async_copy(xbuf.at[0], xbuf.at[0], chain_recv).wait()

    @pl.when(jnp.logical_not(has_before) & (way == 0))
    def _():
        xbuf[0] = edges[0, column]

    @pl.when(jnp.logical_not(has_before) & (way == 1))
    def _():
        xbuf[0] = edges[1, column]

    for u, block in enumerate(unpack_lanes(load_tiles(xbuf, 0, width), chi)):
        x32[u * chi : (u + 1) * chi] = block

    def absorb(step, unused):
        slot = step + way * (group - 1 - 2 * step)

        pending = (step >= 1) & jnp.logical_not(crossing & (step >= local_cols))

        @pl.when(pending & jnp.logical_not(has_before))
        def _():
            prepare(step, 0)

        send_row(
            xbuf.at[step], env_ref.at[way, column], env_send.at[step], env_recv.at[way, column], slot
        )
        x_high, x_low = halves(x32[...])
        q_high = qhi[step]
        jbuf[...] = dot32(x_high, q_high) + (dot32(x_high, qlo[step]) + dot32(x_low, q_high))
        chunk = 16

        def through(at, unused):
            start = pl.multiple_of(at * chunk, chunk)
            for l in range(D2):
                for d in range(D2):
                    total = None
                    for u in range(D2):
                        for w in range(D2):
                            ket_at = (u // D) * 8 + (l // D) * 4 + (d // D) * 2 + w // D
                            bra_at = (u % D) * 8 + (l % D) * 4 + (d % D) * 2 + w % D
                            spot = ket_at * 16 + bra_at
                            term = (
                                ebuf[step, spot : spot + 1, :]
                                * jbuf[
                                    pl.ds(u * chi + start, chunk), w * LANES : (w + 1) * LANES
                                ]
                            )
                            total = term if total is None else total + term
                    high, low = halves(total)
                    rows = pl.ds(l * LANES + start, chunk)
                    thi[rows, d * LANES : (d + 1) * LANES] = high
                    tlo[rows, d * LANES : (d + 1) * LANES] = low
            return unused

        lax.fori_loop(0, chi // chunk, through, 0, unroll=True)
        both = pboth[step]
        large = dot32(both, thi[:, 0:wide])
        renewed = large[:chi] + (large[chi:] + dot32(both[:chi], tlo[:, 0:wide]))
        square = jnp.sum(jnp.sum(renewed * renewed, axis=1, keepdims=True), axis=0, keepdims=True)
        renewed = renewed * (1.0 / jnp.sqrt(square / (chi * width) + EPSILON))
        blocks = [renewed[:, d * LANES : (d + 1) * LANES] for d in range(D2)]
        for d, block in enumerate(blocks):
            x32[d * chi : (d + 1) * chi] = block
        for t, tile in enumerate(pack_lanes(blocks, chi)):
            xbuf[step + 1, :, t * LANES : (t + 1) * LANES] = tile

        @pl.when((step == group - 1) & has_after)
        def _():
            chain_hop.start()

        send_row(
            xbuf.at[step + 1],
            out_ref.at[way, column],
            out_send.at[step],
            out_recv.at[way, column],
            slot,
        )
        return unused

    lax.fori_loop(0, group, absorb, 0)

    unit = jnp.where(
        lax.broadcasted_iota(jnp.int32, (LANES, LANES), 0)
        == lax.broadcasted_iota(jnp.int32, (LANES, LANES), 1),
        1.0,
        0.0,
    ).astype(jnp.bfloat16)
    fill = jnp.zeros((LANES - chi, LANES), jnp.bfloat16)

    def take_boundary(kind):
        for column in range(local_cols):
            landed = env_ref.at[kind, column]
            pltpu.make_async_copy(landed, landed, env_recv.at[kind, column]).wait()
            blocks = unpack_lanes(load_tiles(env_ref.at[kind], column, width), chi)
            for at, block in enumerate(blocks):
                lanes = slice(at * LANES, (at + 1) * LANES)
                for part, values in enumerate(halves(block)):
                    tall_block = jnp.concatenate([values, fill], axis=0)
                    turned = dot_last(unit, tall_block).astype(jnp.bfloat16)
                    if kind == 0:
                        rows = slice(part * chi, (part + 1) * chi)
                        near[0, column, rows, lanes] = turned[:chi]
                        near[1, column, rows, lanes] = values
                    else:
                        far[1, column, part, :, lanes] = turned
                        far[0, column, part, :, lanes] = tall_block

    for turn in range(2):
        for kind in range(2):

            @pl.when((turn + low_half) % 2 == kind)
            def _():
                take_boundary(kind)

    spot_row = lax.broadcasted_iota(jnp.int32, (terms, terms), 0)
    spot_lane = lax.broadcasted_iota(jnp.int32, (terms, terms), 1)

    def stand(ref):
        values = jnp.broadcast_to(ref[...].astype(jnp.float32), (terms, terms))
        return jnp.sum(jnp.where(spot_row == spot_lane, values, 0.0), axis=1, keepdims=True)

    term_row = stand(rows_ref).astype(jnp.int32)
    term_bond = stand(bonds_ref).astype(jnp.int32)
    term_op = stand(ops_ref).astype(jnp.int32)
    term_weights = jnp.zeros((terms, table_ref.shape[1]), jnp.float32)
    for op in range(table_ref.shape[0]):
        term_weights = jnp.where(term_op == op, table_ref[op : op + 1, :], term_weights)

    late = jnp.where(cols_at >= col_count // 2, 1, 0)

    def hop(side, step):
        return pltpu.make_async_remote_copy(
            hop_out.at[side],
            hop_in.at[side],
            hop_send.at[side],
            hop_recv.at[side],
            device_id={"cols": cols_at + step},
        )

    def half_copy(side):
        step = (1, -1)[side]
        return pltpu.make_async_remote_copy(
            half_out.at[side],
            half_in.at[side],
            half_send.at[side],
            half_recv.at[side],
            device_id={"cols": cols_at + step},
        )

    def put_environ(blocks):
        for at, block in enumerate(blocks):
            vbuf[at * chi : (at + 1) * chi] = block

    def walk(turn, unused):
        side = (turn // local_cols + late) % 2
        order = turn % local_cols
        column = order + side * (local_cols - 1 - 2 * order)
        first = ((side == 0) & (cols_at == 0)) | ((side == 1) & (cols_at == col_count - 1))
        final = ((side == 1) & (cols_at == 0)) | ((side == 0) & (cols_at == col_count - 1))
        ending = order == local_cols - 1

        @pl.when((order == 0) & jnp.logical_not(first))
        def _():
            pltpu.make_async_copy(hop_in.at[side], hop_in.at[side], hop_recv.at[side]).wait()
            put_environ(unpack_lanes(load_tiles(hop_in, side, width), chi))

        for at in range(2):

            @pl.when((order == 0) & first & (side == at))
            def _():
                put_environ(unpack_lanes(load_tiles(sides, at, width), chi))

        @pl.when(jnp.logical_not(ending & final))
        def _():
            v_high, v_low = halves(vbuf[...])
            f_high = far[side, column, 0]
            jbuf[...] = dot32(v_high, f_high) + (
                dot32(v_high, far[side, column, 1]) + dot32(v_low, f_high)
            )
            chunk = 16

            def ket(p, u, i, d, o):
                at = p * 16 + u * 8 + i * 4 + d * 2 + o
                return kets_env[side, column, at : at + 1, :]

            def through(at, unused):
                start = pl.multiple_of(at * chunk, chunk)

                def joined(i, d):
                    return jbuf[pl.ds(i * chi + start, chunk), d * LANES : (d + 1) * LANES]

                for p in range(PHYS):
                    for u in range(D):
                        for o in range(D):
                            part = {}
                            for i2 in range(D):
                                for d2 in range(D):
                                    total = None
                                    for i in range(D):
                                        for d in range(D):
                                            term = ket(p, u, i, d, o) * joined(
                                                i * D + i2, d * D + d2
                                            )
                                            total = term if total is None else total + term
                                    part[i2, d2] = total
                            for q in range(PHYS):
                                for u2 in range(D):
                                    for o2 in range(D):
                                        total = None
                                        for i2 in range(D):
                                            for d2 in range(D):
                                                term = ket(q, u2, i2, d2, o2) * part[i2, d2]
                                                total = term if total is None else total + term
                                        high, low = halves(total)
                                        rows = pl.ds((u * D + u2) * LANES + start, chunk)
                                        spot = (p * PHYS + q) * D2 + o * D + o2
                                        lanes = slice(spot * LANES, (spot + 1) * LANES)
                                        thi[rows, lanes] = high
                                        tlo[rows, lanes] = low
                return unused

            lax.fori_loop(0, chi // chunk, through, 0)
            both = near[side, column]
            wide = D2 * LANES
            closed = None
            for pair in range(pairs):
                lanes = slice(pair * wide, (pair + 1) * wide)
                large = dot32(both, thi[:, lanes])
                value = large[:chi] + (large[chi:] + dot32(both[:chi], tlo[:, lanes]))
                opens[side, column, pair] = value
                if pair // PHYS == pair % PHYS:
                    closed = value if closed is None else closed + value
            square = jnp.sum(
                jnp.sum(closed * closed, axis=1, keepdims=True), axis=0, keepdims=True
            )
            closed = closed * (1.0 / jnp.sqrt(square / (chi * width) + EPSILON))
            blocks = [closed[:, d * LANES : (d + 1) * LANES] for d in range(D2)]
            put_environ(blocks)

            @pl.when(ending)
            def _():
                for t, tile in enumerate(pack_lanes(blocks, chi)):
                    hop_out[side, :, t * LANES : (t + 1) * LANES] = tile

            for at, step in enumerate((1, -1)):

                @pl.when(ending & (side == at))
                def _():
                    hop(at, step).start()
                    rows = slice((1 - at) * half, (2 - at) * half)
                    for pair in range(pairs):
                        lanes = [
                            opens[side, column, pair, rows, d * LANES : (d + 1) * LANES]
                            for d in range(D2)
                        ]
                        for t, tile in enumerate(pack_lanes(lanes, chi)):
                            half_out[at, pair, :, t * LANES : (t + 1) * LANES] = tile
                    half_copy(at).start()

        return unused

    lax.fori_loop(0, 2 * local_cols, walk, 0)

    lane = lax.broadcasted_iota(jnp.int32, tall, 1)

    def density(former, latter):
        total = jnp.zeros(tall, jnp.float32)
        for p in range(pairs):
            first = former(p)
            for q in range(pairs):
                value = jnp.sum(
                    jnp.sum(first * latter(q), axis=0, keepdims=True), axis=1, keepdims=True
                )
                total = jnp.where(lane == p * pairs + q, value, total)
        return total

    def share(bond, values):
        hit = (term_row == place) & (term_bond == bond)
        return jnp.where(hit, values, 0.0)

    held = shares.at[cols_at]
    held[...] = jnp.zeros(tall, jnp.float32)
    for column in range(local_cols - 1):
        held[...] += share(
            cols_at * local_cols + column,
            density(lambda p: opens[0, column, p], lambda q: opens[1, column + 1, q]),
        )

    def arrived(side):
        known = {}

        def take(pair):
            if pair not in known:
                known[pair] = jnp.concatenate(
                    unpack_lanes(load_tiles(half_in.at[side], pair, width), chi), axis=1
                )
            return known[pair]

        return take

    def land(side):
        pltpu.make_async_copy(half_in.at[side], half_in.at[side], half_recv.at[side]).wait()

    @pl.when(has_right)
    def _():
        land(1)
        held[...] += share(
            cols_at * local_cols + local_cols - 1,
            density(lambda p: opens[0, local_cols - 1, p, :half], arrived(1)),
        )

    @pl.when(has_left)
    def _():
        land(0)
        held[...] += share(
            cols_at * local_cols - 1,
            density(arrived(0), lambda q: opens[1, 0, q, half:]),
        )

    def spread(buffer, stage, axis, at, count):
        def copies(other):
            return pltpu.make_async_remote_copy(
                buffer.at[at],
                buffer.at[at],
                share_send.at[stage, other],
                share_recv.at[stage, at],
                device_id={axis: other},
            )

        for other in range(count):

            @pl.when(at != other)
            def _():
                copies(other).start()

        for other in range(count):

            @pl.when(at != other)
            def _():
                pltpu.make_async_copy(
                    buffer.at[other], buffer.at[other], share_recv.at[stage, other]
                ).wait()

        total = buffer[0]
        for other in range(1, count):
            total += buffer[other]

        def finish():
            for other in range(count):

                @pl.when(at != other)
                def _():
                    copies(other).wait_send()

        return total, finish

    total, finish_cols = spread(shares, 0, "cols", cols_at, col_count)
    row_share[place] = total
    total, finish_rows = spread(row_share, 1, "rows", place, row_count)
    picked = jnp.sum(total[:, : pairs * pairs] * term_weights, axis=1, keepdims=True)
    bra, ket_at = lane % pairs, lane // pairs
    diagonal = (bra // PHYS == bra % PHYS) & (ket_at // PHYS == ket_at % PHYS)
    trace = jnp.sum(
        jnp.where(diagonal & (lane < pairs * pairs), total, 0.0), axis=1, keepdims=True
    )
    size = jnp.sqrt(jnp.sum(total * total, axis=1, keepdims=True))
    energy = picked / jnp.maximum(jnp.abs(trace), 0.25 * size)
    same = lax.broadcasted_iota(jnp.int32, (terms, terms), 0) == lax.broadcasted_iota(
        jnp.int32, (terms, terms), 1
    )
    energy_ref[...] = jnp.sum(jnp.where(same, energy, 0.0), axis=0, keepdims=True)
    finish_cols()
    finish_rows()

    @pl.when(has_right)
    def _():
        hop(0, 1).wait_send()
        half_copy(0).wait_send()

    @pl.when(has_left)
    def _():
        hop(1, -1).wait_send()
        half_copy(1).wait_send()

    for step in range(group):
        slot = step + way * (group - 1 - 2 * step)

        @pl.when(slot != me)
        def _():
            row_copy(
                xbuf.at[step],
                env_ref.at[way, column],
                env_send.at[step],
                env_recv.at[way, column],
                slot,
            )[0].wait_send()
            row_copy(
                xbuf.at[step + 1],
                out_ref.at[way, column],
                out_send.at[step],
                out_recv.at[way, column],
                slot,
            )[0].wait_send()

    for target in range(group):

        @pl.when(target != me)
        def _():
            for copy in map_copies(target % 2, target // 2, target, False):
                copy.wait_send()

    @pl.when(has_after)
    def _():
        chain_hop.wait_send()

    for a in range(2):
        for b in range(local_cols):
            pltpu.make_async_copy(out_ref.at[a, b], out_ref.at[a, b], out_recv.at[a, b]).wait()


def window(row_count, col_count, args):
    local_cols = args[0].shape[1]
    chi, width = args[1].shape[-2:]
    terms = args[7].shape[0]
    group = 2 * local_cols
    wide = D2 * LANES
    pairs = PHYS * PHYS
    most = max(row_count, col_count)
    entries = args[0].shape[2]
    vmem = pl.BlockSpec(memory_space=pltpu.VMEM)
    stay = pl.BlockSpec(memory_space=pltpu.HBM)
    dma = pltpu.SemaphoreType.DMA

    def f32(*shape):
        return pltpu.VMEM(shape, jnp.float32)

    def bf16(*shape):
        return pltpu.VMEM(shape, jnp.bfloat16)

    return pl.pallas_call(
        functools.partial(window_kernel, row_count, col_count),
        out_shape=(
            jax.ShapeDtypeStruct((2, local_cols, chi, width), jnp.float32),
            jax.ShapeDtypeStruct((1, terms), jnp.float32),
        ),
        in_specs=[vmem] + [stay] * 6 + [vmem] * 4,
        out_specs=(vmem, vmem),
        scratch_shapes=[
            f32(2, local_cols, entries, LANES),
            f32(2, local_cols, entries, LANES),
            f32(2, 2, local_cols, chi, width),
            f32(2, local_cols, chi, width),
            f32(2, chi, width),
            f32(2, local_cols, chi, width),
            f32(group, chi, width),
            f32(group, chi, width),
            f32(group, entries, LANES),
            f32(group + 1, chi, width),
            f32(group, D2**4, LANES),
            bf16(wide, width),
            bf16(group, 2 * chi, wide),
            bf16(group, LANES, wide),
            bf16(group, LANES, wide),
            f32(D2 * chi, LANES),
            f32(D2 * chi, wide),
            bf16(wide, pairs * wide),
            bf16(wide, pairs * wide),
            bf16(2, local_cols, 2 * chi, wide),
            bf16(2, local_cols, 2, LANES, wide),
            f32(D2 * chi, LANES),
            f32(2, local_cols, pairs, chi, wide),
            f32(2, chi, width),
            f32(2, chi, width),
            f32(2, pairs, chi // 2, width),
            f32(2, pairs, chi // 2, width),
            f32(col_count, terms, LANES),
            f32(row_count, terms, LANES),
            dma((6,)),
            dma((3, group)),
            dma((3, group)),
            dma((group,)),
            dma((2, local_cols)),
            dma((group,)),
            dma((2, local_cols)),
            dma,
            dma,
            dma((2,)),
            dma((2,)),
            dma((2,)),
            dma((2,)),
            dma((2, most)),
            dma((2, most)),
        ],
        compiler_params=pltpu.CompilerParams(
            collective_id=0, has_side_effects=True, vmem_limit_bytes=56 * 1024 * 1024
        ),
        name="window",
    )(*args[:7], *(index[None] for index in args[7:10]), args[10])


def shards(*args):
    outs, energies = window(lax.axis_size("rows"), lax.axis_size("cols"), args)
    return (outs[0][None], outs[1][None], energies[0])


def solution(mesh):
    placed = (
        P("rows", "cols", None),
        P(None, "rows", "cols", None, None),
        P(None, "rows", "cols", None, None),
        P("cols", None, None),
        P("cols", None, None),
        P("rows", None, None),
        P("rows", None, None),
        P(),
        P(),
        P(),
        P(),
    )
    return jax.shard_map(
        shards,
        mesh=mesh,
        in_specs=placed,
        out_specs=(P("rows", "cols", None, None), P("rows", "cols", None, None), P()),
        check_vma=False,
    )
```

profile of v0, /device:TPU:0, one launch (start us, length us, event | category | flops | bytes accessed | tf_op | source)
XLA Modules:
  0.0 92.5 jit_solution(1481644647102042174)
XLA Ops:
  0.6 88.8 %window.1 = (f32[2,2,96,384]{3,2,1,0:T(8,128)}, f32[1,16]{1,0:T(1,128)}) custom-call(f32[1,2,32]{2,1,0:T(2,128)} %kets_ref.1, f32[2,1,2,96,384]{4,3,2,1,0:T(8,128)} %left_maps_ref.1, f32[2,1,2,96,384]{4,3,2,1,0:T(8,128)} %right_maps_ref.1, f32[2,96,384]{2,1,0:T(8,128)} %top_ref.1, f32[2,96,384]{2,1,0:T(8,128)} %bottom_ref.1, f32[1,96,384]{2,1,0:T(8,128)} %left_ref.1, ...), custom_call_target="tpu_custom_call" | custom-call | tf_op jit(solution)/shard_map/window/pallas_call | solution.py:763
  89.4 1.9 %fusion = (f32[1,2,96,384]{3,2,1,0:T(8,128)}, f32[1,2,96,384]{3,2,1,0:T(8,128)}) fusion(f32[2,2,96,384]{3,2,1,0:T(8,128)} %get-tuple-element.5), kind=kLoop, calls=%fused_computation | loop fusion | bytes 1179648 | tf_op jit(solution)/shard_map/slice | solution.py:826
  91.4 0.0 copy-start
  91.4 0.6 copy-done
  91.9 0.5 copy.15
Async XLA Ops:
  91.4 0.6 copy-start
where the time goes:
time: 92.7 us; the launch traced here: 92.5 us
  Pallas kernels  88.8 us (96%)
  local copies, waits for them, and re-layouts  3.01 us (3%)
    pallas_call x1, Pallas kernels, window(): pl.pallas_call(functools.partial(window_kernel, row_count, col_count), ou...  88.8 us
    slice x1, local copies, waits for them, and re-layouts, shards(): return (outs[0][None], outs[1][None], energies[0])  1.9 us

commit v1 on v0

--- a/solution.py
+++ b/solution.py
@@ -119,6 +119,7 @@
     half_in,
     shares,
     row_share,
+    token,
     load_sem,
     map_send,
     map_recv,
@@ -159,11 +160,22 @@
     has_after = (after >= 0) & (after < groups)
 
     barrier = pltpu.get_barrier_semaphore()
-    for other in range(row_count):
-
-        @pl.when(place != other)
-        def _():
-            pl.semaphore_signal(barrier, inc=1, device_id={"rows": other})
+    for other in range(group):
+
+        @pl.when(me != other)
+        def _():
+            pl.semaphore_signal(barrier, inc=1, device_id={"rows": base + other})
+
+    has_lower = mine > 0
+    has_upper = mine < groups - 1
+
+    @pl.when(has_lower)
+    def _():
+        pl.semaphore_signal(barrier, inc=1, device_id={"rows": place - group})
+
+    @pl.when(has_upper)
+    def _():
+        pl.semaphore_signal(barrier, inc=1, device_id={"rows": place + group})
 
     for other in range(col_count):
 
@@ -216,7 +228,21 @@
     tlo[...] = jnp.zeros_like(tlo)
     for load in loads:
         load.wait()
-    pl.semaphore_wait(barrier, row_count - 1 + col_count - 1)
+    greeted = jnp.where(has_lower, 1, 0) + jnp.where(has_upper, 1, 0)
+    pl.semaphore_wait(barrier, group - 1 + col_count - 1 + greeted)
+
+    def pass_token(way_at):
+        pl.semaphore_signal(
+            token.at[way_at], inc=1, device_id={"rows": place + (group, -group)[way_at]}
+        )
+
+    @pl.when(has_upper & jnp.logical_not(has_lower))
+    def _():
+        pass_token(0)
+
+    @pl.when(has_lower & jnp.logical_not(has_upper))
+    def _():
+        pass_token(1)
 
     def map_copies(target_way, target_col, target, local):
         made = []
@@ -320,6 +346,12 @@
 
     lax.fori_loop(0, ahead, prepare_ahead, 0)
 
+    @pl.when(has_lower & has_upper)
+    def _():
+        for way_at in range(2):
+            pl.semaphore_wait(token.at[way_at], 1)
+            pass_token(way_at)
+
     @pl.when(has_before)
     def _():
         pltpu.make_async_copy(xbuf.at[0], xbuf.at[0], chain_recv).wait()
@@ -678,8 +710,6 @@
         return total, finish
 
     total, finish_cols = spread(shares, 0, "cols", cols_at, col_count)
-    row_share[place] = total
-    total, finish_rows = spread(row_share, 1, "rows", place, row_count)
     picked = jnp.sum(total[:, : pairs * pairs] * term_weights, axis=1, keepdims=True)
     bra, ket_at = lane % pairs, lane // pairs
     diagonal = (bra // PHYS == bra % PHYS) & (ket_at // PHYS == ket_at % PHYS)
@@ -688,10 +718,21 @@
     )
     size = jnp.sqrt(jnp.sum(total * total, axis=1, keepdims=True))
     energy = picked / jnp.maximum(jnp.abs(trace), 0.25 * size)
-    same = lax.broadcasted_iota(jnp.int32, (terms, terms), 0) == lax.broadcasted_iota(
-        jnp.int32, (terms, terms), 1
+    same = lax.broadcasted_iota(jnp.int32, tall, 0) == lane
+    row_share[place] = jnp.sum(
+        jnp.where(same & (term_row == place), energy, 0.0), axis=0, keepdims=True
     )
-    energy_ref[...] = jnp.sum(jnp.where(same, energy, 0.0), axis=0, keepdims=True)
+
+    @pl.when(has_lower & jnp.logical_not(has_upper))
+    def _():
+        pl.semaphore_wait(token.at[0], 1)
+
+    @pl.when(has_upper & jnp.logical_not(has_lower))
+    def _():
+        pl.semaphore_wait(token.at[1], 1)
+
+    total, finish_rows = spread(row_share, 1, "rows", place, row_count)
+    energy_ref[...] = total[:, :terms]
     finish_cols()
     finish_rows()
 
@@ -797,7 +838,8 @@
             f32(2, pairs, chi // 2, width),
             f32(2, pairs, chi // 2, width),
             f32(col_count, terms, LANES),
-            f32(row_count, terms, LANES),
+            f32(row_count, 1, LANES),
+            pltpu.SemaphoreType.REGULAR((2,)),
             dma((6,)),
             dma((3, group)),
             dma((3, group)),

time: 92.7 us -> 89.8 us (0.969)
  Pallas kernels: 88.8 us -> 85.9 us
    pallas_call x1, Pallas kernels: 88.8 us -> 85.9 us  [window(): pl.pallas_call(functools.partial(window_kernel, row_count, col_count), ou...]
where the time goes in v1:
time: 89.8 us; the launch traced here: 89.6 us
  Pallas kernels  85.9 us (96%)
  local copies, waits for them, and re-layouts  3.01 us (3%)
    pallas_call x1, Pallas kernels, window(): pl.pallas_call(functools.partial(window_kernel, row_count, col_count), ou...  85.9 us
    slice x1, local copies, waits for them, and re-layouts, shards(): return (outs[0][None], outs[1][None], energies[0])  1.9 us

profile of v1, /device:TPU:0, one launch (start us, length us, event | category | flops | bytes accessed | tf_op | source)
XLA Modules:
  0.0 89.6 jit_solution(6989613317553563587)
XLA Ops:
  0.6 85.9 %window.1 = (f32[2,2,96,384]{3,2,1,0:T(8,128)}, f32[1,16]{1,0:T(1,128)}) custom-call(f32[1,2,32]{2,1,0:T(2,128)} %kets_ref.1, f32[2,1,2,96,384]{4,3,2,1,0:T(8,128)} %left_maps_ref.1, f32[2,1,2,96,384]{4,3,2,1,0:T(8,128)} %right_maps_ref.1, f32[2,96,384]{2,1,0:T(8,128)} %top_ref.1, f32[2,96,384]{2,1,0:T(8,128)} %bottom_ref.1, f32[1,96,384]{2,1,0:T(8,128)} %left_ref.1, ...), custom_call_target="tpu_custom_call" | custom-call | tf_op jit(solution)/shard_map/window/pallas_call | solution.py:804
  86.5 1.9 %fusion = (f32[1,2,96,384]{3,2,1,0:T(8,128)}, f32[1,2,96,384]{3,2,1,0:T(8,128)}) fusion(f32[2,2,96,384]{3,2,1,0:T(8,128)} %get-tuple-element.5), kind=kLoop, calls=%fused_computation | loop fusion | bytes 1179648 | tf_op jit(solution)/shard_map/slice | solution.py:868
  88.5 0.0 copy-start
  88.5 0.6 copy-done
  89.0 0.5 copy.15
Async XLA Ops:
  88.5 0.6 copy-start

commit v2 on v1

v2 whole, which is shorter than its diff:
```python
import functools

import jax
import jax.numpy as jnp
from jax import lax
from jax.experimental import pallas as pl
from jax.experimental.pallas import tpu as pltpu
from jax.sharding import PartitionSpec as P

D = 2
D2 = 4
PHYS = 2
EPSILON = 1e-06
LANES = 128


def unpack_lanes(tiles, chi):
    rolled = {}
    lane = lax.broadcasted_iota(jnp.int32, tiles[0].shape, 1)
    blocks = []
    for block in range(D2):
        total = jnp.zeros_like(tiles[0])
        for place, tile in enumerate(tiles):
            low = max(chi * block, LANES * place)
            high = min(chi * (block + 1), LANES * (place + 1))
            if low >= high:
                continue
            shift = (LANES * place - chi * block) % LANES
            if (place, shift) not in rolled:
                rolled[place, shift] = tile if shift == 0 else pltpu.roll(tile, shift, 1)
            inside = (lane >= low - chi * block) & (lane < high - chi * block)
            total = jnp.where(inside, rolled[place, shift], total)
        blocks.append(total)
    return blocks


def pack_lanes(blocks, chi):
    lane = lax.broadcasted_iota(jnp.int32, blocks[0].shape, 1)
    rolled = {}
    tiles = []
    for place in range(chi * D2 // LANES):
        total = jnp.zeros_like(blocks[0])
        for block, values in enumerate(blocks):
            low = max(chi * block, LANES * place)
            high = min(chi * (block + 1), LANES * (place + 1))
            if low >= high:
                continue
            shift = (chi * block - LANES * place) % LANES
            if (block, shift) not in rolled:
                rolled[block, shift] = values if shift == 0 else pltpu.roll(values, shift, 1)
            inside = (lane >= low - LANES * place) & (lane < high - LANES * place)
            total = jnp.where(inside, rolled[block, shift], total)
        tiles.append(total)
    return tiles


def halves(values):
    high = values.astype(jnp.bfloat16)
    low = (values - high.astype(jnp.float32)).astype(jnp.bfloat16)
    return high, low


def dot32(former, latter):
    return jnp.dot(former, latter, preferred_element_type=jnp.float32)


def dot_last(former, latter):
    return lax.dot_general(
        former, latter, (((1,), (1,)), ((), ())), preferred_element_type=jnp.float32
    )


def load_tiles(ref, at, width):
    return [ref[at, :, LANES * t : LANES * (t + 1)] for t in range(width // LANES)]


def window_kernel(
    row_count,
    col_count,
    kets_ref,
    left_maps_ref,
    right_maps_ref,
    top_ref,
    bottom_ref,
    left_ref,
    right_ref,
    rows_ref,
    bonds_ref,
    ops_ref,
    table_ref,
    out_ref,
    energy_ref,
    kets,
    kets_near,
    maps,
    edges,
    sides,
    env_ref,
    pbuf,
    qbuf,
    kbuf,
    xbuf,
    ebuf,
    pick,
    turn_pick,
    pmap,
    rbuf,
    fold,
    xw,
    jbuf,
    thi,
    tlo,
    near,
    far,
    vbuf,
    opens,
    hop_out,
    hop_in,
    share,
    shared,
    token,
    load_sem,
    map_send,
    map_recv,
    env_send,
    side_send,
    env_recv,
    out_send,
    out_recv,
    chain_send,
    chain_recv,
    hop_send,
    hop_recv,
    share_send,
    share_recv,
    ket_send,
    ket_recv,
):
    local_cols = kets.shape[1]
    chi, width = maps.shape[3], maps.shape[4]
    wide = D2 * LANES
    pairs = PHYS * PHYS
    terms = rows_ref.shape[1]
    group = 2 * local_cols
    groups = row_count // group
    place = lax.axis_index("rows")
    cols_at = lax.axis_index("cols")
    has_left = cols_at > 0
    has_right = cols_at < col_count - 1
    mine = place // group
    me = place % group
    column = me // 2
    way = me % 2
    base = mine * group
    before = mine - 1 + 2 * way
    after = mine + 1 - 2 * way
    has_before = (before >= 0) & (before < groups)
    has_after = (after >= 0) & (after < groups)
    low_half = jnp.where(mine >= groups // 2, 1, 0)
    early, late = low_half, 1 - low_half
    has_lower = mine > 0
    has_upper = mine < groups - 1

    barrier = pltpu.get_barrier_semaphore()
    for at in range(col_count):
        for other in range(group):

            @pl.when((me != other) | (cols_at != at))
            def _():
                pl.semaphore_signal(
                    barrier, inc=1, device_id={"rows": base + other, "cols": at}
                )

    @pl.when(has_lower)
    def _():
        pl.semaphore_signal(barrier, inc=1, device_id={"rows": place - group})

    @pl.when(has_upper)
    def _():
        pl.semaphore_signal(barrier, inc=1, device_id={"rows": place + group})

    loads = [
        pltpu.make_async_copy(source, target, load_sem.at[at])
        for at, (source, target) in enumerate(
            (
                (right_maps_ref.at[:, 0], maps.at[0]),
                (left_maps_ref.at[:, 0], maps.at[1]),
                (top_ref, edges.at[0]),
                (bottom_ref, edges.at[1]),
                (left_ref, sides.at[pl.ds(0, 1)]),
                (right_ref, sides.at[pl.ds(1, 1)]),
            )
        )
    ]
    for load in loads:
        load.start()

    count = kets_ref.shape[2]
    spot = lax.broadcasted_iota(jnp.int32, (count, count), 0)
    from_lane = lax.broadcasted_iota(jnp.int32, (count, count), 1)

    def exchanged(high, low):
        top, bottom = (spot // high) % 2, (spot // low) % 2
        return spot + (bottom - top) * high + (top - bottom) * low

    def led(out, into):
        rest = (spot // 8) % 2 * 16 + (spot // 2) % 2 * 4 + spot % 2
        return rest + spot // 16 * out + (spot // 4) % 2 * into

    for order, ref, target in (
        (led(2, 8), kets, 0),
        (led(8, 2), kets, 1),
        (spot + (exchanged(8, 2) - spot) * late, kets_near, 0),
        (spot + (exchanged(8, 2) - spot) * late + (exchanged(4, 1) - spot), kets_near, 1),
    ):
        for at in range(local_cols):
            values = jnp.broadcast_to(kets_ref[0, at : at + 1, :], (count, count))
            tallest = jnp.sum(
                jnp.where(order == from_lane, values, 0.0), axis=1, keepdims=True
            )
            filled = jnp.broadcast_to(tallest, (count, LANES))
            if ref is kets:
                kets[target, at] = filled
            else:
                kets_near[at + 1, target] = filled

    chosen = lax.broadcasted_iota(jnp.int32, (wide, width), 0)
    entry = lax.broadcasted_iota(jnp.int32, (wide, width), 1)
    wanted = (chosen % LANES) * D2 + chosen // LANES
    live = (chosen % LANES) < chi
    pick[...] = jnp.where((wanted == entry) & live, 1.0, 0.0).astype(jnp.bfloat16)
    chosen = lax.broadcasted_iota(jnp.int32, (width, width), 0)
    entry = lax.broadcasted_iota(jnp.int32, (width, width), 1)
    wanted = (chosen % chi) * D2 + chosen // chi
    turn_pick[...] = jnp.where(wanted == entry, 1.0, 0.0).astype(jnp.bfloat16)
    xw[...] = jnp.zeros_like(xw)
    thi[...] = jnp.zeros_like(thi)
    tlo[...] = jnp.zeros_like(tlo)
    for load in loads:
        load.wait()
    greeted = jnp.where(has_lower, 1, 0) + jnp.where(has_upper, 1, 0)
    pl.semaphore_wait(barrier, group * col_count - 1 + greeted)

    def pass_token(way_at):
        pl.semaphore_signal(
            token.at[way_at], inc=1, device_id={"rows": place + (group, -group)[way_at]}
        )

    @pl.when(has_upper & jnp.logical_not(has_lower))
    def _():
        pass_token(0)

    @pl.when(has_lower & jnp.logical_not(has_upper))
    def _():
        pass_token(1)

    ket_copy = pltpu.make_async_remote_copy(
        kets_near.at[local_cols],
        kets_near.at[0],
        ket_send,
        ket_recv,
        device_id={"cols": cols_at + 1},
    )

    @pl.when(has_right)
    def _():
        ket_copy.start()

    def map_copies(target_way, target_col, target, local):
        made = []
        for kind, (source, buffer) in enumerate(
            ((kets, kbuf), (maps.at[0], qbuf), (maps.at[1], pbuf))
        ):
            origin, landing = source.at[target_way, target_col], buffer.at[me]
            if local:
                made.append(pltpu.make_async_copy(origin, landing, map_recv.at[kind, me]))
            else:
                made.append(
                    pltpu.make_async_remote_copy(
                        origin,
                        landing,
                        map_send.at[kind, target],
                        map_recv.at[kind, me],
                        device_id={"rows": base + target},
                    )
                )
        return made

    for turn in range(group):
        target_way = (low_half + turn // local_cols) % 2
        target_col = turn % local_cols
        target = target_col * 2 + target_way

        @pl.when(target != me)
        def _():
            for copy in map_copies(target_way, target_col, target, False):
                copy.start()

        @pl.when(target == me)
        def _():
            for copy in map_copies(target_way, target_col, target, True):
                copy.start()

    lane_pair = lax.broadcasted_iota(jnp.int32, (count // 2, width), 1) // chi

    def folded_kets(values):
        former, latter = (
            jnp.concatenate([part] * (width // LANES), axis=1)
            for part in (values[: count // 2], values[count // 2 :])
        )
        ket = jnp.where(lane_pair // D == 0, former, latter)
        bra = jnp.where(lane_pair % D == 0, former, latter)
        legs = D**3
        for i in range(legs):
            total = ket[i : i + 1] * bra[:legs]
            for p in range(1, PHYS):
                total += ket[p * legs + i : p * legs + i + 1] * bra[p * legs : (p + 1) * legs]
            ebuf[i * legs : (i + 1) * legs] = total

    def fold_into(target):
        chunk = 16

        def through(at, unused):
            start = pl.multiple_of(at * chunk, chunk)
            tiles = [rbuf[pl.ds(c * chi + start, chunk), :] for c in range(D2)]
            for g in range(D2):
                for h in range(D2):
                    total = None
                    for c, tile in enumerate(tiles):
                        ket_at = (h // D) * 4 + (g // D) * 2 + c // D
                        bra_at = (h % D) * 4 + (g % D) * 2 + c % D
                        spot = ket_at * D**3 + bra_at
                        term = ebuf[spot : spot + 1, :] * tile
                        total = term if total is None else total + term
                    high, low = halves(total)
                    rows = pl.ds((g * D2 + h) * chi + start, chunk)
                    target[rows, :width] = high
                    target[rows, width:] = low
            return unused

        lax.fori_loop(0, chi // chunk, through, 0)

    def put_right(values):
        high, low = halves(values)
        xw[:chi] = high
        xw[LANES : LANES + chi] = low

    def joined_with(high, low):
        return dot32(jnp.concatenate([high, high], axis=1), xw[...]) + dot32(low, xw[:LANES])

    def absorbed(joined, folded):
        rows = []
        for part in halves(joined):
            rows.append(
                jnp.concatenate([part[g * chi : (g + 1) * chi] for g in range(D2)], axis=1)
            )
        large = dot32(jnp.concatenate(rows, axis=0), folded)
        high, low = large[:, :width], large[:, width:]
        return high[:chi] + ((high[chi:] + low[:chi]) + low[chi:])

    def normalized(values):
        square = jnp.sum(jnp.sum(values * values, axis=1, keepdims=True), axis=0, keepdims=True)
        return values * (1.0 / jnp.sqrt(square / (chi * width) + EPSILON))

    def prepare(step, unused):
        slot = step + way * (group - 1 - 2 * step)
        for kind, buffer in enumerate((kbuf, qbuf, pbuf)):
            pltpu.make_async_copy(
                buffer.at[slot], buffer.at[slot], map_recv.at[kind, slot]
            ).wait()
        folded_kets(kbuf[slot])
        for at, part in enumerate(halves(pbuf[slot])):
            spread_map = dot_last(part, pick[...]).astype(jnp.bfloat16)
            for l in range(D2):
                pmap[step, at, l * chi : (l + 1) * chi] = spread_map[
                    :, l * LANES : (l + 1) * LANES
                ]
        high, low = (
            dot_last(turn_pick[...], jnp.concatenate([part] * D2, axis=0))
            for part in halves(qbuf[slot])
        )
        rbuf[...] = high + low
        fold_into(fold.at[step])
        return unused

    def row_copy(source, landing, send, recv, slot):
        remote = pltpu.make_async_remote_copy(
            source, landing, send, recv, device_id={"rows": base + slot}
        )
        return remote, pltpu.make_async_copy(source, landing, recv)

    def send_row(source, landing, send, recv, slot):
        remote, local = row_copy(source, landing, send, recv, slot)

        @pl.when(slot != me)
        def _():
            remote.start()

        @pl.when(slot == me)
        def _():
            local.start()

    chain_hop = pltpu.make_async_remote_copy(
        xbuf.at[group],
        xbuf.at[0],
        chain_send,
        chain_recv,
        device_id={"rows": after * group + me},
    )

    start_slot = way * (group - 1)
    crossing = jnp.logical_not(has_before) & ((start_slot // local_cols) != (me // local_cols))
    ahead = jnp.where(has_before, group, jnp.where(crossing, group - local_cols + 1, 1))
    turned_by = jnp.where(crossing, local_cols, 0)

    def prepare_ahead(turn, unused):
        return prepare((turn + turned_by) % group, unused)

    lax.fori_loop(0, ahead, prepare_ahead, 0)

    @pl.when(has_lower & has_upper)
    def _():
        for way_at in range(2):
            pl.semaphore_wait(token.at[way_at], 1)
            pass_token(way_at)

    def side_copy(step, slot):
        return pltpu.make_async_remote_copy(
            xbuf.at[step],
            env_ref.at[way, 0],
            side_send.at[step],
            env_recv.at[way, 0],
            device_id={"rows": base + slot, "cols": cols_at + 1},
        )

    def absorb(step, unused):
        slot = step + way * (group - 1 - 2 * step)

        pending = (step >= 1) & jnp.logical_not(crossing & (step >= local_cols))

        @pl.when(pending & jnp.logical_not(has_before))
        def _():
            prepare(step, 0)

        send_row(
            xbuf.at[step],
            env_ref.at[way, column + 1],
            env_send.at[step],
            env_recv.at[way, column + 1],
            slot,
        )

        @pl.when(has_right & (column == local_cols - 1))
        def _():
            side_copy(step, slot).start()

        joined = joined_with(pmap[step, 0], pmap[step, 1])
        renewed = normalized(absorbed(joined, fold[step]))
        xbuf[step + 1] = renewed
        put_right(renewed)

        @pl.when((step == group - 1) & has_after)
        def _():
            chain_hop.start()

        return unused

    def run_chain():
        @pl.when(has_before)
        def _():
            pltpu.make_async_copy(xbuf.at[0], xbuf.at[0], chain_recv).wait()

        @pl.when(jnp.logical_not(has_before) & (way == 0))
        def _():
            xbuf[0] = edges[0, column]

        @pl.when(jnp.logical_not(has_before) & (way == 1))
        def _():
            xbuf[0] = edges[1, column]

        put_right(xbuf[0])
        lax.fori_loop(0, group, absorb, 0)

        for step in range(group):
            send_row(
                xbuf.at[step + 1],
                out_ref.at[way, column],
                out_send.at[step],
                out_recv.at[way, column],
                step + way * (group - 1 - 2 * step),
            )

    unit = jnp.where(
        lax.broadcasted_iota(jnp.int32, (LANES, LANES), 0)
        == lax.broadcasted_iota(jnp.int32, (LANES, LANES), 1),
        1.0,
        0.0,
    ).astype(jnp.bfloat16)
    fill = jnp.zeros((LANES - chi, LANES), jnp.bfloat16)

    def take_blocks(kind, at):
        landed = env_ref.at[kind, at]
        pltpu.make_async_copy(landed, landed, env_recv.at[kind, at]).wait()
        blocks = unpack_lanes(load_tiles(env_ref.at[kind], at, width), chi)
        for d, block in enumerate(blocks):
            lanes = slice(d * LANES, (d + 1) * LANES)
            for part, values in enumerate(halves(block)):
                tall_block = jnp.concatenate([values, fill], axis=0)
                turned = dot_last(unit, tall_block).astype(jnp.bfloat16)
                yield lanes, part, values, tall_block, turned

    def take_far(at):
        for lanes, part, values, tall_block, turned in take_blocks(early, at):
            far[1, at, part, :, lanes] = turned
            far[0, at, part, :, lanes] = tall_block

    def take_near(at):
        for lanes, part, values, tall_block, turned in take_blocks(late, at):
            rows = slice(part * chi, (part + 1) * chi)
            near[0, at, rows, lanes] = turned[:chi]
            near[1, at, rows, lanes] = values

    def for_columns(take):
        for at in range(1, local_cols + 1):
            take(at)

        @pl.when(has_left)
        def _():
            take(0)

    second = jnp.where(cols_at >= col_count // 2, 1, 0)

    def hop(side, step):
        return pltpu.make_async_remote_copy(
            hop_out.at[side],
            hop_in.at[side],
            hop_send.at[side],
            hop_recv.at[side],
            device_id={"cols": cols_at + step},
        )

    def put_environ(blocks):
        for at, block in enumerate(blocks):
            vbuf[at * chi : (at + 1) * chi] = block

    def put_edge(side):
        blocks = unpack_lanes(load_tiles(sides, side, width), chi)

        @pl.when(late == 0)
        def _():
            put_environ(blocks)

        @pl.when(late == 1)
        def _():
            empty = jnp.zeros((LANES - chi, LANES), jnp.float32)
            put_environ([jnp.concatenate([block, empty], axis=0).T[:chi] for block in blocks])

    def place_of(side, order):
        return order + side * (local_cols - 2 * order)

    def open_up(side, at_column):
        v_high, v_low = halves(vbuf[...])
        f_high = far[side, at_column, 0]
        jbuf[...] = dot32(v_high, f_high) + (
            dot32(v_high, far[side, at_column, 1]) + dot32(v_low, f_high)
        )
        chunk = 16

        def ket(p, u, i, d, o):
            at = p * 16 + u * 8 + i * 4 + d * 2 + o
            return kets_near[at_column, side, at : at + 1, :]

        def through(at, unused):
            start = pl.multiple_of(at * chunk, chunk)

            def joined(i, d):
                return jbuf[pl.ds(i * chi + start, chunk), d * LANES : (d + 1) * LANES]

            for p in range(PHYS):
                for u in range(D):
                    for o in range(D):
                        part = {}
                        for i2 in range(D):
                            for d2 in range(D):
                                total = None
                                for i in range(D):
                                    for d in range(D):
                                        term = ket(p, u, i, d, o) * joined(
                                            i * D + i2, d * D + d2
                                        )
                                        total = term if total is None else total + term
                                part[i2, d2] = total
                        for q in range(PHYS):
                            for u2 in range(D):
                                for o2 in range(D):
                                    total = None
                                    for i2 in range(D):
                                        for d2 in range(D):
                                            term = ket(q, u2, i2, d2, o2) * part[i2, d2]
                                            total = term if total is None else total + term
                                    high, low = halves(total)
                                    rows = pl.ds((u * D + u2) * LANES + start, chunk)
                                    spot = (p * PHYS + q) * D2 + o * D + o2
                                    lanes = slice(spot * LANES, (spot + 1) * LANES)
                                    thi[rows, lanes] = high
                                    tlo[rows, lanes] = low
            return unused

        lax.fori_loop(0, chi // chunk, through, 0)

    def first_order(side):
        return jnp.where((side == 0) & (cols_at == 0), 1, 0)

    def is_edge(side):
        return ((side == 0) & (cols_at == 0)) | ((side == 1) & (cols_at == col_count - 1))

    def early_work():
        @pl.when(has_left)
        def _():
            pltpu.make_async_copy(kets_near.at[0], kets_near.at[0], ket_recv).wait()

        for_columns(take_far)
        for side in range(2):

            @pl.when(is_edge(side))
            def _():
                put_edge(side)

        @pl.when(is_edge(second))
        def _():
            open_up(second, place_of(second, first_order(second)))

    early_first = (way != low_half) & (mine != groups // 2) & (mine != groups // 2 - 1)
    early_at = jnp.where(early_first, 0, 1)

    def phase(at, unused):
        @pl.when(at == early_at)
        def _():
            early_work()

        @pl.when(at != early_at)
        def _():
            run_chain()

        return unused

    lax.fori_loop(0, 2, phase, 0)
    for_columns(take_near)

    spot_row = lax.broadcasted_iota(jnp.int32, (terms, terms), 0)
    spot_lane = lax.broadcasted_iota(jnp.int32, (terms, terms), 1)

    def stand(ref):
        values = jnp.broadcast_to(ref[...].astype(jnp.float32), (terms, terms))
        return jnp.sum(jnp.where(spot_row == spot_lane, values, 0.0), axis=1, keepdims=True)

    term_row = stand(rows_ref).astype(jnp.int32)
    term_bond = stand(bonds_ref).astype(jnp.int32)
    term_op = stand(ops_ref).astype(jnp.int32)
    term_weights = jnp.zeros((terms, table_ref.shape[1]), jnp.float32)
    for op in range(table_ref.shape[0]):
        term_weights = jnp.where(term_op == op, table_ref[op : op + 1, :], term_weights)

    def walk(turn, unused):
        side = (turn // local_cols + second) % 2
        order = turn % local_cols
        at_column = place_of(side, order)
        absent = (cols_at == 0) & (at_column == side)
        opening = order == first_order(side)
        ending = order == local_cols - 1

        @pl.when((order == 0) & jnp.logical_not(is_edge(side)))
        def _():
            pltpu.make_async_copy(hop_in.at[side], hop_in.at[side], hop_recv.at[side]).wait()
            put_environ(unpack_lanes(load_tiles(hop_in, side, width), chi))

        @pl.when(jnp.logical_not(absent) & jnp.logical_not(opening & is_edge(side)))
        def _():
            open_up(side, at_column)

        @pl.when(jnp.logical_not(absent))
        def _():
            both = near[side, at_column]
            closed = None
            for pair in range(pairs):
                lanes = slice(pair * wide, (pair + 1) * wide)
                large = dot32(both, thi[:, lanes])
                value = large[:chi] + (large[chi:] + dot32(both[:chi], tlo[:, lanes]))
                opens[side, at_column - side, pair] = value
                if pair // PHYS == pair % PHYS:
                    closed = value if closed is None else closed + value
            square = jnp.sum(
                jnp.sum(closed * closed, axis=1, keepdims=True), axis=0, keepdims=True
            )
            closed = closed * (1.0 / jnp.sqrt(square / (chi * width) + EPSILON))
            blocks = [closed[:, d * LANES : (d + 1) * LANES] for d in range(D2)]
            put_environ(blocks)

            @pl.when(ending)
            def _():
                for t, tile in enumerate(pack_lanes(blocks, chi)):
                    hop_out[side, :, t * LANES : (t + 1) * LANES] = tile

        @pl.when(ending & (side == 0) & has_right)
        def _():
            hop(0, 1).start()

        @pl.when(ending & (side == 1) & has_left)
        def _():
            hop(1, -1).start()

        return unused

    lax.fori_loop(0, 2 * local_cols, walk, 0)

    tall = (terms, LANES)
    lane = lax.broadcasted_iota(jnp.int32, tall, 1)
    held = shared.at[0]
    held[...] = jnp.zeros(tall, jnp.float32)
    here = jnp.zeros((terms, 1), jnp.int32)
    for k in range(local_cols):
        bond = cols_at * local_cols + k - 1
        hit = (term_row == place) & (term_bond == bond)
        here = jnp.where(hit, 1, here)

        def add_bond(k=k, hit=hit):
            values = jnp.zeros(tall, jnp.float32)
            for p in range(pairs):
                former = opens[0, k, p]
                for q in range(pairs):
                    value = jnp.sum(
                        jnp.sum(former * opens[1, k, q], axis=0, keepdims=True),
                        axis=1,
                        keepdims=True,
                    )
                    values = jnp.where(lane == p * pairs + q, value, values)
            held[...] += jnp.where(hit, values, 0.0)

        if k:
            add_bond()
        else:
            pl.when(has_left)(add_bond)

    total = held[...]
    picked = jnp.sum(total[:, : pairs * pairs] * term_weights, axis=1, keepdims=True)
    bra, ket_at = lane % pairs, lane // pairs
    diagonal = (bra // PHYS == bra % PHYS) & (ket_at // PHYS == ket_at % PHYS)
    trace = jnp.sum(
        jnp.where(diagonal & (lane < pairs * pairs), total, 0.0), axis=1, keepdims=True
    )
    size = jnp.sqrt(jnp.sum(total * total, axis=1, keepdims=True))
    energy = picked / jnp.maximum(jnp.abs(trace), 0.25 * size)
    same = lax.broadcasted_iota(jnp.int32, tall, 0) == lane
    devices = row_count * col_count
    spot_mine = place * col_count + cols_at
    own = share.at[devices]
    own[...] = jnp.sum(jnp.where(same & (here == 1), energy, 0.0), axis=0, keepdims=True)

    @pl.when(has_lower & jnp.logical_not(has_upper))
    def _():
        pl.semaphore_wait(token.at[0], 1)

    @pl.when(has_upper & jnp.logical_not(has_lower))
    def _():
        pl.semaphore_wait(token.at[1], 1)

    def tell(other, unused):
        @pl.when(other != spot_mine)
        def _():
            pltpu.make_async_remote_copy(
                own,
                share.at[spot_mine],
                share_send,
                share_recv,
                device_id={"rows": other // col_count, "cols": other % col_count},
            ).start()

        return unused

    lax.fori_loop(0, devices, tell, 0)
    pltpu.make_async_copy(own, share.at[spot_mine], share_recv).start()
    everyone = share.at[pl.ds(0, devices)]
    pltpu.make_async_copy(everyone, everyone, share_recv).wait()
    energy_ref[...] = jnp.sum(share[:devices], axis=0)[:, :terms]
    others = share.at[pl.ds(0, devices - 1)]
    pltpu.make_async_copy(others, others, share_send).wait()

    @pl.when(has_right)
    def _():
        hop(0, 1).wait_send()
        ket_copy.wait_send()

    @pl.when(has_left)
    def _():
        hop(1, -1).wait_send()

    for step in range(group):
        slot = step + way * (group - 1 - 2 * step)

        @pl.when(slot != me)
        def _():
            row_copy(
                xbuf.at[step],
                env_ref.at[way, column + 1],
                env_send.at[step],
                env_recv.at[way, column + 1],
                slot,
            )[0].wait_send()
            row_copy(
                xbuf.at[step + 1],
                out_ref.at[way, column],
                out_send.at[step],
                out_recv.at[way, column],
                slot,
            )[0].wait_send()

        @pl.when(has_right & (column == local_cols - 1))
        def _():
            side_copy(step, slot).wait_send()

    for target in range(group):

        @pl.when(target != me)
        def _():
            for copy in map_copies(target % 2, target // 2, target, False):
                copy.wait_send()

    @pl.when(has_after)
    def _():
        chain_hop.wait_send()

    for a in range(2):
        for b in range(local_cols):
            pltpu.make_async_copy(out_ref.at[a, b], out_ref.at[a, b], out_recv.at[a, b]).wait()


def window(row_count, col_count, args):
    local_cols = args[0].shape[1]
    chi, width = args[1].shape[-2:]
    terms = args[7].shape[0]
    group = 2 * local_cols
    wide = D2 * LANES
    pairs = PHYS * PHYS
    entries = args[0].shape[2]
    vmem = pl.BlockSpec(memory_space=pltpu.VMEM)
    stay = pl.BlockSpec(memory_space=pltpu.HBM)
    dma = pltpu.SemaphoreType.DMA

    def f32(*shape):
        return pltpu.VMEM(shape, jnp.float32)

    def bf16(*shape):
        return pltpu.VMEM(shape, jnp.bfloat16)

    return pl.pallas_call(
        functools.partial(window_kernel, row_count, col_count),
        out_shape=(
            jax.ShapeDtypeStruct((2, local_cols, chi, width), jnp.float32),
            jax.ShapeDtypeStruct((1, terms), jnp.float32),
        ),
        in_specs=[vmem] + [stay] * 6 + [vmem] * 4,
        out_specs=(vmem, vmem),
        scratch_shapes=[
            f32(2, local_cols, entries, LANES),
            f32(local_cols + 1, 2, entries, LANES),
            f32(2, 2, local_cols, chi, width),
            f32(2, local_cols, chi, width),
            f32(2, chi, width),
            f32(2, local_cols + 1, chi, width),
            f32(group, chi, width),
            f32(group, chi, width),
            f32(group, entries, LANES),
            f32(group + 1, chi, width),
            f32(D2**3, width),
            bf16(wide, width),
            bf16(width, width),
            bf16(group, 2, width, LANES),
            f32(width, width),
            bf16(group, D2 * width, 2 * width),
            bf16(2 * LANES, width),
            f32(D2 * chi, wide),
            bf16(wide, pairs * wide),
            bf16(wide, pairs * wide),
            bf16(2, local_cols + 1, 2 * chi, wide),
            bf16(2, local_cols + 1, 2, LANES, wide),
            f32(D2 * chi, LANES),
            f32(2, local_cols, pairs, chi, wide),
            f32(2, chi, width),
            f32(2, chi, width),
            f32(row_count * col_count + 1, 1, LANES),
            f32(1, terms, LANES),
            pltpu.SemaphoreType.REGULAR((2,)),
            dma((6,)),
            dma((3, group)),
            dma((3, group)),
            dma((group,)),
            dma((group,)),
            dma((2, local_cols + 1)),
            dma((group,)),
            dma((2, local_cols)),
            dma,
            dma,
            dma((2,)),
            dma((2,)),
            dma,
            dma,
            dma,
            dma,
        ],
        compiler_params=pltpu.CompilerParams(
            collective_id=0, has_side_effects=True, vmem_limit_bytes=56 * 1024 * 1024
        ),
        name="window",
    )(*args[:7], *(index[None] for index in args[7:10]), args[10])


def shards(*args):
    outs, energies = window(lax.axis_size("rows"), lax.axis_size("cols"), args)
    return (outs[0][None], outs[1][None], energies[0])


def solution(mesh):
    placed = (
        P("rows", "cols", None),
        P(None, "rows", "cols", None, None),
        P(None, "rows", "cols", None, None),
        P("cols", None, None),
        P("cols", None, None),
        P("rows", None, None),
        P("rows", None, None),
        P(),
        P(),
        P(),
        P(),
    )
    return jax.shard_map(
        shards,
        mesh=mesh,
        in_specs=placed,
        out_specs=(P("rows", "cols", None, None), P("rows", "cols", None, None), P()),
        check_vma=False,
    )
```

time: 89.8 us -> 77.6 us (0.86)
  Pallas kernels: 85.9 us -> 73.8 us
    pallas_call x1, Pallas kernels: 85.9 us -> 73.8 us  [window(): pl.pallas_call(functools.partial(window_kernel, row_count, col_count), ou...]
where the time goes in v2:
time: 77.6 us; the launch traced here: 77.4 us
  Pallas kernels  73.8 us (95%)
  local copies, waits for them, and re-layouts  3.01 us (4%)
    pallas_call x1, Pallas kernels, window(): pl.pallas_call(functools.partial(window_kernel, row_count, col_count), ou...  73.8 us
    slice x1, local copies, waits for them, and re-layouts, shards(): return (outs[0][None], outs[1][None], energies[0])  1.9 us

profile of v2, /device:TPU:0, one launch (start us, length us, event | category | flops | bytes accessed | tf_op | source)
XLA Modules:
  0.0 77.4 jit_solution(69879969490884678)
XLA Ops:
  0.6 73.8 %window.1 = (f32[2,2,96,384]{3,2,1,0:T(8,128)}, f32[1,16]{1,0:T(1,128)}) custom-call(f32[1,2,32]{2,1,0:T(2,128)} %kets_ref.1, f32[2,1,2,96,384]{4,3,2,1,0:T(8,128)} %left_maps_ref.1, f32[2,1,2,96,384]{4,3,2,1,0:T(8,128)} %right_maps_ref.1, f32[2,96,384]{2,1,0:T(8,128)} %top_ref.1, f32[2,96,384]{2,1,0:T(8,128)} %bottom_ref.1, f32[1,96,384]{2,1,0:T(8,128)} %left_ref.1, ...), custom_call_target="tpu_custom_call" | custom-call | tf_op jit(solution)/shard_map/window/pallas_call | solution.py:855
  74.4 1.9 %fusion = (f32[1,2,96,384]{3,2,1,0:T(8,128)}, f32[1,2,96,384]{3,2,1,0:T(8,128)}) fusion(f32[2,2,96,384]{3,2,1,0:T(8,128)} %get-tuple-element.5), kind=kLoop, calls=%fused_computation | loop fusion | bytes 1179648 | tf_op jit(solution)/shard_map/slice | solution.py:919
  76.3 0.0 copy-start
  76.3 0.6 copy-done
  76.9 0.5 copy.15
Async XLA Ops:
  76.3 0.6 copy-start

commit v3 on v2

--- a/solution.py
+++ b/solution.py
@@ -12,6 +12,7 @@
 PHYS = 2
 EPSILON = 1e-06
 LANES = 128
+PACE = 9
 
 
 def unpack_lanes(tiles, chi):
@@ -145,8 +146,6 @@
     groups = row_count // group
     place = lax.axis_index("rows")
     cols_at = lax.axis_index("cols")
-    has_left = cols_at > 0
-    has_right = cols_at < col_count - 1
     mine = place // group
     me = place % group
     column = me // 2
@@ -158,6 +157,17 @@
     has_after = (after >= 0) & (after < groups)
     low_half = jnp.where(mine >= groups // 2, 1, 0)
     early, late = low_half, 1 - low_half
+    onward = 1 - 2 * late
+    rank = cols_at + late * (col_count - 1 - 2 * cols_at)
+    has_prev = rank > 0
+    has_next = rank < col_count - 1
+    edge_col = low_half * (local_cols - 1)
+
+    def spot_of(at):
+        return at + 1 + late * (local_cols - 1 - 2 * at)
+
+    def true_side(side):
+        return side + late * (1 - 2 * side)
     has_lower = mine > 0
     has_upper = mine < groups - 1
 
@@ -222,10 +232,10 @@
             if ref is kets:
                 kets[target, at] = filled
             else:
-                kets_near[at + 1, target] = filled
-
-    chosen = lax.broadcasted_iota(jnp.int32, (wide, width), 0)
-    entry = lax.broadcasted_iota(jnp.int32, (wide, width), 1)
+                kets_near[spot_of(at), target] = filled
+
+    chosen = lax.broadcasted_iota(jnp.int32, (width, wide), 1)
+    entry = lax.broadcasted_iota(jnp.int32, (width, wide), 0)
     wanted = (chosen % LANES) * D2 + chosen // LANES
     live = (chosen % LANES) < chi
     pick[...] = jnp.where((wanted == entry) & live, 1.0, 0.0).astype(jnp.bfloat16)
@@ -234,8 +244,6 @@
     wanted = (chosen % chi) * D2 + chosen // chi
     turn_pick[...] = jnp.where(wanted == entry, 1.0, 0.0).astype(jnp.bfloat16)
     xw[...] = jnp.zeros_like(xw)
-    thi[...] = jnp.zeros_like(thi)
-    tlo[...] = jnp.zeros_like(tlo)
     for load in loads:
         load.wait()
     greeted = jnp.where(has_lower, 1, 0) + jnp.where(has_upper, 1, 0)
@@ -259,10 +267,10 @@
         kets_near.at[0],
         ket_send,
         ket_recv,
-        device_id={"cols": cols_at + 1},
+        device_id={"cols": cols_at + onward},
     )
 
-    @pl.when(has_right)
+    @pl.when(has_next)
     def _():
         ket_copy.start()
 
@@ -286,20 +294,56 @@
                 )
         return made
 
-    for turn in range(group):
-        target_way = (low_half + turn // local_cols) % 2
-        target_col = turn % local_cols
-        target = target_col * 2 + target_way
-
-        @pl.when(target != me)
-        def _():
-            for copy in map_copies(target_way, target_col, target, False):
-                copy.start()
-
-        @pl.when(target == me)
-        def _():
-            for copy in map_copies(target_way, target_col, target, True):
-                copy.start()
+    def each_map(target_way, cross, act):
+        for target_col in range(local_cols):
+            target = target_col * 2 + target_way
+            wanted = (target_col != column) if cross else (target_col == column)
+
+            @pl.when(wanted & (target != me))
+            def _():
+                for copy in map_copies(target_way, target_col, target, False):
+                    act(copy, False)
+
+            @pl.when(wanted & (target == me))
+            def _():
+                for copy in map_copies(target_way, target_col, target, True):
+                    act(copy, True)
+
+    def start(copy, local):
+        copy.start()
+
+    def finish(copy, local):
+        if not local:
+            copy.wait_send()
+
+    opening_chain = jnp.logical_not(has_before)
+
+    def start_later_maps():
+        for cross in (True, False):
+            each_map(late, cross, start)
+
+    each_map(low_half, False, start)
+    leading = me % 2 == low_half
+
+    @pl.when(leading)
+    def _():
+        each_map(low_half, True, start)
+
+    def clear(at, unused):
+        thi[...] = jnp.zeros_like(thi)
+        tlo[...] = jnp.zeros_like(tlo)
+        return unused
+
+    lax.fori_loop(0, jnp.where(leading, 1, PACE), clear, 0)
+
+    @pl.when(jnp.logical_not(leading))
+    def _():
+        each_map(low_half, True, start)
+
+    @pl.when(has_before)
+    def _():
+        each_map(low_half, True, finish)
+        start_later_maps()
 
     lane_pair = lax.broadcasted_iota(jnp.int32, (count // 2, width), 1) // chi
 
@@ -319,6 +363,7 @@
 
     def fold_into(target):
         chunk = 16
+        full = width // (2 * LANES) * 2 * LANES
 
         def through(at, unused):
             start = pl.multiple_of(at * chunk, chunk)
@@ -335,7 +380,8 @@
                     high, low = halves(total)
                     rows = pl.ds((g * D2 + h) * chi + start, chunk)
                     target[rows, :width] = high
-                    target[rows, width:] = low
+                    target[rows, width : 2 * width - full] = low[:, full:]
+                    target[rows, 2 * width - full :] = low[:, :full]
             return unused
 
         lax.fori_loop(0, chi // chunk, through, 0)
@@ -348,15 +394,27 @@
     def joined_with(high, low):
         return dot32(jnp.concatenate([high, high], axis=1), xw[...]) + dot32(low, xw[:LANES])
 
-    def absorbed(joined, folded):
-        rows = []
-        for part in halves(joined):
-            rows.append(
-                jnp.concatenate([part[g * chi : (g + 1) * chi] for g in range(D2)], axis=1)
-            )
-        large = dot32(jnp.concatenate(rows, axis=0), folded)
-        high, low = large[:, :width], large[:, width:]
-        return high[:chi] + ((high[chi:] + low[:chi]) + low[chi:])
+    def absorbed(at_step):
+        full = width // (2 * LANES) * 2 * LANES
+        part = D2 * chi // 2
+        joined = [
+            joined_with(pmap[at_step, 0, at : at + part], pmap[at_step, 1, at : at + part])
+            for at in (0, part)
+        ]
+        total = None
+        for at, piece in enumerate(joined):
+            rows = [
+                jnp.concatenate([half[g * chi : (g + 1) * chi] for g in range(D2 // 2)], axis=1)
+                for half in halves(piece)
+            ]
+            depth = slice(at * D2 // 2 * width, (at + 1) * D2 // 2 * width)
+            large = dot32(jnp.concatenate(rows, axis=0), fold[at_step, depth, : 2 * width - full])
+            front = large[:chi, :width] + large[chi:, :width]
+            rest = large[:chi, width:] + large[chi:, width:]
+            small = dot32(rows[0], fold[at_step, depth, 2 * width - full :])
+            value = jnp.concatenate([front[:, :full] + small, front[:, full:] + rest], axis=1)
+            total = value if total is None else total + value
+        return total
 
     def normalized(values):
         square = jnp.sum(jnp.sum(values * values, axis=1, keepdims=True), axis=0, keepdims=True)
@@ -369,17 +427,20 @@
                 buffer.at[slot], buffer.at[slot], map_recv.at[kind, slot]
             ).wait()
         folded_kets(kbuf[slot])
-        for at, part in enumerate(halves(pbuf[slot])):
-            spread_map = dot_last(part, pick[...]).astype(jnp.bfloat16)
+        gap = jnp.zeros((LANES - chi, width), jnp.bfloat16)
+        high, low = halves(qbuf[slot])
+        turned = dot_last(turn_pick[...], jnp.concatenate([high, gap, low, gap], axis=0))
+        turned = turned[:, :LANES] + turned[:, LANES:]
+        for t, tile in enumerate(pack_lanes([turned] * D2, chi)):
+            rbuf[:, t * LANES : (t + 1) * LANES] = tile
+        spread_map = dot32(
+            jnp.concatenate(halves(pbuf[slot]), axis=0), pick[...]
+        ).astype(jnp.bfloat16)
+        for at in range(2):
             for l in range(D2):
                 pmap[step, at, l * chi : (l + 1) * chi] = spread_map[
-                    :, l * LANES : (l + 1) * LANES
+                    at * chi : (at + 1) * chi, l * LANES : (l + 1) * LANES
                 ]
-        high, low = (
-            dot_last(turn_pick[...], jnp.concatenate([part] * D2, axis=0))
-            for part in halves(qbuf[slot])
-        )
-        rbuf[...] = high + low
         fold_into(fold.at[step])
         return unused
 
@@ -416,7 +477,6 @@
     def prepare_ahead(turn, unused):
         return prepare((turn + turned_by) % group, unused)
 
-    lax.fori_loop(0, ahead, prepare_ahead, 0)
 
     @pl.when(has_lower & has_upper)
     def _():
@@ -430,12 +490,16 @@
             env_ref.at[way, 0],
             side_send.at[step],
             env_recv.at[way, 0],
-            device_id={"rows": base + slot, "cols": cols_at + 1},
+            device_id={"rows": base + slot, "cols": cols_at + onward},
         )
 
     def absorb(step, unused):
         slot = step + way * (group - 1 - 2 * step)
 
+        @pl.when(opening_chain & (step == local_cols))
+        def _():
+            start_later_maps()
+
         pending = (step >= 1) & jnp.logical_not(crossing & (step >= local_cols))
 
         @pl.when(pending & jnp.logical_not(has_before))
@@ -444,18 +508,17 @@
 
         send_row(
             xbuf.at[step],
-            env_ref.at[way, column + 1],
+            env_ref.at[way, spot_of(column)],
             env_send.at[step],
-            env_recv.at[way, column + 1],
+            env_recv.at[way, spot_of(column)],
             slot,
         )
 
-        @pl.when(has_right & (column == local_cols - 1))
+        @pl.when(has_next & (column == edge_col))
         def _():
             side_copy(step, slot).start()
 
-        joined = joined_with(pmap[step, 0], pmap[step, 1])
-        renewed = normalized(absorbed(joined, fold[step]))
+        renewed = normalized(absorbed(step))
         xbuf[step + 1] = renewed
         put_right(renewed)
 
@@ -466,6 +529,8 @@
         return unused
 
     def run_chain():
+        lax.fori_loop(0, ahead, prepare_ahead, 0)
+
         @pl.when(has_before)
         def _():
             pltpu.make_async_copy(xbuf.at[0], xbuf.at[0], chain_recv).wait()
@@ -520,23 +585,15 @@
             near[0, at, rows, lanes] = turned[:chi]
             near[1, at, rows, lanes] = values
 
-    def for_columns(take):
-        for at in range(1, local_cols + 1):
-            take(at)
-
-        @pl.when(has_left)
-        def _():
-            take(0)
-
-    second = jnp.where(cols_at >= col_count // 2, 1, 0)
-
-    def hop(side, step):
+    second = jnp.where(rank >= col_count // 2, 1, 0)
+
+    def hop(side):
         return pltpu.make_async_remote_copy(
             hop_out.at[side],
             hop_in.at[side],
             hop_send.at[side],
             hop_recv.at[side],
-            device_id={"cols": cols_at + step},
+            device_id={"cols": cols_at + onward * (1 - 2 * side)},
         )
 
     def put_environ(blocks):
@@ -544,7 +601,7 @@
             vbuf[at * chi : (at + 1) * chi] = block
 
     def put_edge(side):
-        blocks = unpack_lanes(load_tiles(sides, side, width), chi)
+        blocks = unpack_lanes(load_tiles(sides, true_side(side), width), chi)
 
         @pl.when(late == 0)
         def _():
@@ -560,15 +617,16 @@
 
     def open_up(side, at_column):
         v_high, v_low = halves(vbuf[...])
-        f_high = far[side, at_column, 0]
+        true = true_side(side)
+        f_high = far[true, at_column, 0]
         jbuf[...] = dot32(v_high, f_high) + (
-            dot32(v_high, far[side, at_column, 1]) + dot32(v_low, f_high)
+            dot32(v_high, far[true, at_column, 1]) + dot32(v_low, f_high)
         )
         chunk = 16
 
         def ket(p, u, i, d, o):
             at = p * 16 + u * 8 + i * 4 + d * 2 + o
-            return kets_near[at_column, side, at : at + 1, :]
+            return kets_near[at_column, true, at : at + 1, :]
 
         def through(at, unused):
             start = pl.multiple_of(at * chunk, chunk)
@@ -609,17 +667,23 @@
         lax.fori_loop(0, chi // chunk, through, 0)
 
     def first_order(side):
-        return jnp.where((side == 0) & (cols_at == 0), 1, 0)
+        return jnp.where((side == 0) & (rank == 0), 1, 0)
 
     def is_edge(side):
-        return ((side == 0) & (cols_at == 0)) | ((side == 1) & (cols_at == col_count - 1))
+        return ((side == 0) & (rank == 0)) | ((side == 1) & (rank == col_count - 1))
 
     def early_work():
-        @pl.when(has_left)
+        @pl.when(has_prev)
         def _():
             pltpu.make_async_copy(kets_near.at[0], kets_near.at[0], ket_recv).wait()
 
-        for_columns(take_far)
+        for at in range(1, local_cols + 1):
+            take_far(at)
+
+        @pl.when(has_prev)
+        def _():
+            take_far(0)
+
         for side in range(2):
 
             @pl.when(is_edge(side))
@@ -645,7 +709,8 @@
         return unused
 
     lax.fori_loop(0, 2, phase, 0)
-    for_columns(take_near)
+    for at in range(1, local_cols + 1):
+        take_near(at)
 
     spot_row = lax.broadcasted_iota(jnp.int32, (terms, terms), 0)
     spot_lane = lax.broadcasted_iota(jnp.int32, (terms, terms), 1)
@@ -665,7 +730,7 @@
         side = (turn // local_cols + second) % 2
         order = turn % local_cols
         at_column = place_of(side, order)
-        absent = (cols_at == 0) & (at_column == side)
+        absent = (rank == 0) & (at_column == side)
         opening = order == first_order(side)
         ending = order == local_cols - 1
 
@@ -678,15 +743,19 @@
         def _():
             open_up(side, at_column)
 
+        @pl.when(jnp.logical_not(absent) & (at_column == 0))
+        def _():
+            take_near(0)
+
         @pl.when(jnp.logical_not(absent))
         def _():
-            both = near[side, at_column]
+            both = near[true_side(side), at_column]
             closed = None
             for pair in range(pairs):
                 lanes = slice(pair * wide, (pair + 1) * wide)
                 large = dot32(both, thi[:, lanes])
                 value = large[:chi] + (large[chi:] + dot32(both[:chi], tlo[:, lanes]))
-                opens[side, at_column - side, pair] = value
+                opens[true_side(side), at_column - side, pair] = value
                 if pair // PHYS == pair % PHYS:
                     closed = value if closed is None else closed + value
             square = jnp.sum(
@@ -701,13 +770,13 @@
                 for t, tile in enumerate(pack_lanes(blocks, chi)):
                     hop_out[side, :, t * LANES : (t + 1) * LANES] = tile
 
-        @pl.when(ending & (side == 0) & has_right)
-        def _():
-            hop(0, 1).start()
-
-        @pl.when(ending & (side == 1) & has_left)
-        def _():
-            hop(1, -1).start()
+        @pl.when(ending & (side == 0) & has_next)
+        def _():
+            hop(0).start()
+
+        @pl.when(ending & (side == 1) & has_prev)
+        def _():
+            hop(1).start()
 
         return unused
 
@@ -719,7 +788,7 @@
     held[...] = jnp.zeros(tall, jnp.float32)
     here = jnp.zeros((terms, 1), jnp.int32)
     for k in range(local_cols):
-        bond = cols_at * local_cols + k - 1
+        bond = cols_at * local_cols + k - 1 + late * (local_cols - 2 * k)
         hit = (term_row == place) & (term_bond == bond)
         here = jnp.where(hit, 1, here)
 
@@ -739,7 +808,7 @@
         if k:
             add_bond()
         else:
-            pl.when(has_left)(add_bond)
+            pl.when(has_prev)(add_bond)
 
     total = held[...]
     picked = jnp.sum(total[:, : pairs * pairs] * term_weights, axis=1, keepdims=True)
@@ -764,20 +833,23 @@
     def _():
         pl.semaphore_wait(token.at[1], 1)
 
-    def tell(other, unused):
-        @pl.when(other != spot_mine)
-        def _():
-            pltpu.make_async_remote_copy(
-                own,
-                share.at[spot_mine],
-                share_send,
-                share_recv,
-                device_id={"rows": other // col_count, "cols": other % col_count},
-            ).start()
+    def tell(turn, unused):
+        row = turn + late * (row_count - 1 - 2 * turn)
+        for col in range(col_count):
+
+            @pl.when((row != place) | (col != cols_at))
+            def _():
+                pltpu.make_async_remote_copy(
+                    own,
+                    share.at[spot_mine],
+                    share_send,
+                    share_recv,
+                    device_id={"rows": row, "cols": col},
+                ).start()
 
         return unused
 
-    lax.fori_loop(0, devices, tell, 0)
+    lax.fori_loop(0, row_count, tell, 0)
     pltpu.make_async_copy(own, share.at[spot_mine], share_recv).start()
     everyone = share.at[pl.ds(0, devices)]
     pltpu.make_async_copy(everyone, everyone, share_recv).wait()
@@ -785,14 +857,14 @@
     others = share.at[pl.ds(0, devices - 1)]
     pltpu.make_async_copy(others, others, share_send).wait()
 
-    @pl.when(has_right)
-    def _():
-        hop(0, 1).wait_send()
+    @pl.when(has_next)
+    def _():
+        hop(0).wait_send()
         ket_copy.wait_send()
 
-    @pl.when(has_left)
-    def _():
-        hop(1, -1).wait_send()
+    @pl.when(has_prev)
+    def _():
+        hop(1).wait_send()
 
     for step in range(group):
         slot = step + way * (group - 1 - 2 * step)
@@ -801,9 +873,9 @@
         def _():
             row_copy(
                 xbuf.at[step],
-                env_ref.at[way, column + 1],
+                env_ref.at[way, spot_of(column)],
                 env_send.at[step],
-                env_recv.at[way, column + 1],
+                env_recv.at[way, spot_of(column)],
                 slot,
             )[0].wait_send()
             row_copy(
@@ -814,16 +886,17 @@
                 slot,
             )[0].wait_send()
 
-        @pl.when(has_right & (column == local_cols - 1))
+        @pl.when(has_next & (column == edge_col))
         def _():
             side_copy(step, slot).wait_send()
 
-    for target in range(group):
-
-        @pl.when(target != me)
-        def _():
-            for copy in map_copies(target % 2, target // 2, target, False):
-                copy.wait_send()
+    @pl.when(opening_chain)
+    def _():
+        each_map(low_half, True, finish)
+
+    each_map(low_half, False, finish)
+    for cross in (True, False):
+        each_map(late, cross, finish)
 
     @pl.when(has_after)
     def _():
@@ -859,7 +932,7 @@
             jax.ShapeDtypeStruct((1, terms), jnp.float32),
         ),
         in_specs=[vmem] + [stay] * 6 + [vmem] * 4,
-        out_specs=(vmem, vmem),
+        out_specs=(stay, vmem),
         scratch_shapes=[
             f32(2, local_cols, entries, LANES),
             f32(local_cols + 1, 2, entries, LANES),
@@ -872,7 +945,7 @@
             f32(group, entries, LANES),
             f32(group + 1, chi, width),
             f32(D2**3, width),
-            bf16(wide, width),
+            bf16(width, wide),
             bf16(width, width),
             bf16(group, 2, width, LANES),
             f32(width, width),

time: 77.6 us -> 70.7 us (0.911)
  Pallas kernels: 73.8 us -> 66.8 us
    pallas_call x1, Pallas kernels: 73.8 us -> 66.8 us  [window(): pl.pallas_call(functools.partial(window_kernel, row_count, col_count), ou...]
where the time goes in v3:
time: 70.7 us; the launch traced here: 70.5 us
  Pallas kernels  66.8 us (94%)
  local copies, waits for them, and re-layouts  3.01 us (4%)
    pallas_call x1, Pallas kernels, window(): pl.pallas_call(functools.partial(window_kernel, row_count, col_count), ou...  66.8 us
    slice x1, local copies, waits for them, and re-layouts, shards(): return (outs[0][None], outs[1][None], energies[0])  1.9 us

profile of v3, /device:TPU:0, one launch (start us, length us, event | category | flops | bytes accessed | tf_op | source)
XLA Modules:
  0.0 70.5 jit_solution(14216607786861817667)
XLA Ops:
  0.6 66.8 %window.1 = (f32[2,2,96,384]{3,2,1,0:T(8,128)}, f32[1,16]{1,0:T(1,128)}) custom-call(f32[1,2,32]{2,1,0:T(2,128)} %kets_ref.1, f32[2,1,2,96,384]{4,3,2,1,0:T(8,128)} %left_maps_ref.1, f32[2,1,2,96,384]{4,3,2,1,0:T(8,128)} %right_maps_ref.1, f32[2,96,384]{2,1,0:T(8,128)} %top_ref.1, f32[2,96,384]{2,1,0:T(8,128)} %bottom_ref.1, f32[1,96,384]{2,1,0:T(8,128)} %left_ref.1, ...), custom_call_target="tpu_custom_call" | custom-call | tf_op jit(solution)/shard_map/window/pallas_call | solution.py:928
  67.5 1.9 %fusion = (f32[1,2,96,384]{3,2,1,0:T(8,128)}, f32[1,2,96,384]{3,2,1,0:T(8,128)}) fusion(f32[2,2,96,384]{3,2,1,0:T(8,128)} %get-tuple-element.5), kind=kLoop, calls=%fused_computation | loop fusion | bytes 1179648 | tf_op jit(solution)/shard_map/slice | solution.py:992
  69.4 0.0 copy-start
  69.4 0.6 copy-done
  70.0 0.5 copy.15
Async XLA Ops:
  69.4 0.6 copy-start

commit v4 on v3

--- a/solution.py
+++ b/solution.py
@@ -90,7 +90,7 @@
     ops_ref,
     table_ref,
     out_ref,
-    energy_ref,
+    share,
     kets,
     kets_near,
     maps,
@@ -117,7 +117,7 @@
     opens,
     hop_out,
     hop_in,
-    share,
+    own_share,
     shared,
     token,
     load_sem,
@@ -388,17 +388,19 @@
 
     def put_right(values):
         high, low = halves(values)
-        xw[:chi] = high
-        xw[LANES : LANES + chi] = low
-
-    def joined_with(high, low):
-        return dot32(jnp.concatenate([high, high], axis=1), xw[...]) + dot32(low, xw[:LANES])
+        xw[:chi, :width] = high
+        xw[LANES : LANES + chi, :width] = high
+        xw[:chi, width:] = low
+
+    def joined_with(maps):
+        both = dot32(maps, xw[...])
+        return both[:, :width] + both[:, width:]
 
     def absorbed(at_step):
         full = width // (2 * LANES) * 2 * LANES
         part = D2 * chi // 2
         joined = [
-            joined_with(pmap[at_step, 0, at : at + part], pmap[at_step, 1, at : at + part])
+            joined_with(pmap[at_step, at : at + part])
             for at in (0, part)
         ]
         total = None
@@ -416,9 +418,9 @@
             total = value if total is None else total + value
         return total
 
-    def normalized(values):
+    def size_of(values):
         square = jnp.sum(jnp.sum(values * values, axis=1, keepdims=True), axis=0, keepdims=True)
-        return values * (1.0 / jnp.sqrt(square / (chi * width) + EPSILON))
+        return square / (chi * width)
 
     def prepare(step, unused):
         slot = step + way * (group - 1 - 2 * step)
@@ -438,7 +440,8 @@
         ).astype(jnp.bfloat16)
         for at in range(2):
             for l in range(D2):
-                pmap[step, at, l * chi : (l + 1) * chi] = spread_map[
+                lanes = slice(at * LANES, (at + 1) * LANES)
+                pmap[step, l * chi : (l + 1) * chi, lanes] = spread_map[
                     at * chi : (at + 1) * chi, l * LANES : (l + 1) * LANES
                 ]
         fold_into(fold.at[step])
@@ -493,7 +496,8 @@
             device_id={"rows": base + slot, "cols": cols_at + onward},
         )
 
-    def absorb(step, unused):
+    def absorb(step, carried):
+        known, ratio = carried
         slot = step + way * (group - 1 - 2 * step)
 
         @pl.when(opening_chain & (step == local_cols))
@@ -518,15 +522,16 @@
         def _():
             side_copy(step, slot).start()
 
-        renewed = normalized(absorbed(step))
-        xbuf[step + 1] = renewed
-        put_right(renewed)
+        renewed = absorbed(step)
+        put_right(renewed * known)
+        factor = ratio * lax.rsqrt(ratio * ratio * size_of(renewed) + EPSILON)
+        xbuf[step + 1] = renewed * factor
 
         @pl.when((step == group - 1) & has_after)
         def _():
             chain_hop.start()
 
-        return unused
+        return factor, factor / known
 
     def run_chain():
         lax.fori_loop(0, ahead, prepare_ahead, 0)
@@ -544,7 +549,8 @@
             xbuf[0] = edges[1, column]
 
         put_right(xbuf[0])
-        lax.fori_loop(0, group, absorb, 0)
+        one = jnp.ones((1, 1), jnp.float32)
+        lax.fori_loop(0, group, absorb, (one, one))
 
         for step in range(group):
             send_row(
@@ -576,8 +582,10 @@
 
     def take_far(at):
         for lanes, part, values, tall_block, turned in take_blocks(early, at):
-            far[1, at, part, :, lanes] = turned
-            far[0, at, part, :, lanes] = tall_block
+            for copy in (0, 1) if part == 0 else (2,):
+                rows = slice(copy * LANES, (copy + 1) * LANES)
+                far[1, at, rows, lanes] = turned
+                far[0, at, rows, lanes] = tall_block
 
     def take_near(at):
         for lanes, part, values, tall_block, turned in take_blocks(late, at):
@@ -615,56 +623,68 @@
     def place_of(side, order):
         return order + side * (local_cols - 2 * order)
 
-    def open_up(side, at_column):
+    def join(side, at_column):
         v_high, v_low = halves(vbuf[...])
         true = true_side(side)
-        f_high = far[true, at_column, 0]
-        jbuf[...] = dot32(v_high, f_high) + (
-            dot32(v_high, far[true, at_column, 1]) + dot32(v_low, f_high)
-        )
-        chunk = 16
+        jbuf[...] = dot32(
+            jnp.concatenate([v_high, v_low], axis=1), far[true, at_column, : 2 * LANES]
+        ) + dot32(v_high, far[true, at_column, 2 * LANES :])
+
+    chunk = 16
+
+    def pass_through(side, at_column, p, start):
+        true = true_side(side)
 
         def ket(p, u, i, d, o):
             at = p * 16 + u * 8 + i * 4 + d * 2 + o
             return kets_near[at_column, true, at : at + 1, :]
 
+        def joined(i, d):
+            return jbuf[pl.ds(i * chi + start, chunk), d * LANES : (d + 1) * LANES]
+
+        for u in range(D):
+            for o in range(D):
+                part = {}
+                for i2 in range(D):
+                    for d2 in range(D):
+                        total = None
+                        for i in range(D):
+                            for d in range(D):
+                                term = ket(p, u, i, d, o) * joined(i * D + i2, d * D + d2)
+                                total = term if total is None else total + term
+                        part[i2, d2] = total
+                for q in range(PHYS):
+                    for u2 in range(D):
+                        for o2 in range(D):
+                            total = None
+                            for i2 in range(D):
+                                for d2 in range(D):
+                                    term = ket(q, u2, i2, d2, o2) * part[i2, d2]
+                                    total = term if total is None else total + term
+                            high, low = halves(total)
+                            rows = pl.ds((u * D + u2) * LANES + start, chunk)
+                            spot = (p * PHYS + q) * D2 + o * D + o2
+                            lanes = slice(spot * LANES, (spot + 1) * LANES)
+                            thi[rows, lanes] = high
+                            tlo[rows, lanes] = low
+
+    def open_up(side, at_column):
+        join(side, at_column)
+
         def through(at, unused):
-            start = pl.multiple_of(at * chunk, chunk)
-
-            def joined(i, d):
-                return jbuf[pl.ds(i * chi + start, chunk), d * LANES : (d + 1) * LANES]
-
             for p in range(PHYS):
-                for u in range(D):
-                    for o in range(D):
-                        part = {}
-                        for i2 in range(D):
-                            for d2 in range(D):
-                                total = None
-                                for i in range(D):
-                                    for d in range(D):
-                                        term = ket(p, u, i, d, o) * joined(
-                                            i * D + i2, d * D + d2
-                                        )
-                                        total = term if total is None else total + term
-                                part[i2, d2] = total
-                        for q in range(PHYS):
-                            for u2 in range(D):
-                                for o2 in range(D):
-                                    total = None
-                                    for i2 in range(D):
-                                        for d2 in range(D):
-                                            term = ket(q, u2, i2, d2, o2) * part[i2, d2]
-                                            total = term if total is None else total + term
-                                    high, low = halves(total)
-                                    rows = pl.ds((u * D + u2) * LANES + start, chunk)
-                                    spot = (p * PHYS + q) * D2 + o * D + o2
-                                    lanes = slice(spot * LANES, (spot + 1) * LANES)
-                                    thi[rows, lanes] = high
-                                    tlo[rows, lanes] = low
+                pass_through(side, at_column, p, pl.multiple_of(at * chunk, chunk))
             return unused
 
         lax.fori_loop(0, chi // chunk, through, 0)
+
+    def close(side, at_column, pair):
+        both = near[true_side(side), at_column]
+        lanes = slice(pair * wide, (pair + 1) * wide)
+        large = dot32(both, thi[:, lanes])
+        opens[true_side(side), at_column - side, pair] = large[:chi] + (
+            large[chi:] + dot32(both[:chi], tlo[:, lanes])
+        )
 
     def first_order(side):
         return jnp.where((side == 0) & (rank == 0), 1, 0)
@@ -739,25 +759,29 @@
             pltpu.make_async_copy(hop_in.at[side], hop_in.at[side], hop_recv.at[side]).wait()
             put_environ(unpack_lanes(load_tiles(hop_in, side, width), chi))
 
+        @pl.when(jnp.logical_not(absent) & (at_column == 0))
+        def _():
+            take_near(0)
+
+        @pl.when(jnp.logical_not(absent) & opening & is_edge(side))
+        def _():
+            for pair in range(pairs):
+                close(side, at_column, pair)
+
         @pl.when(jnp.logical_not(absent) & jnp.logical_not(opening & is_edge(side)))
         def _():
-            open_up(side, at_column)
-
-        @pl.when(jnp.logical_not(absent) & (at_column == 0))
-        def _():
-            take_near(0)
+            join(side, at_column)
+            for p in range(PHYS):
+                for start in range(0, chi, chunk):
+                    pass_through(side, at_column, p, start)
+                for q in range(PHYS):
+                    close(side, at_column, p * PHYS + q)
 
         @pl.when(jnp.logical_not(absent))
         def _():
-            both = near[true_side(side), at_column]
-            closed = None
-            for pair in range(pairs):
-                lanes = slice(pair * wide, (pair + 1) * wide)
-                large = dot32(both, thi[:, lanes])
-                value = large[:chi] + (large[chi:] + dot32(both[:chi], tlo[:, lanes]))
-                opens[true_side(side), at_column - side, pair] = value
-                if pair // PHYS == pair % PHYS:
-                    closed = value if closed is None else closed + value
+            closed = opens[true_side(side), at_column - side, 0]
+            for p in range(1, PHYS):
+                closed += opens[true_side(side), at_column - side, p * PHYS + p]
             square = jnp.sum(
                 jnp.sum(closed * closed, axis=1, keepdims=True), axis=0, keepdims=True
             )
@@ -822,7 +846,7 @@
     same = lax.broadcasted_iota(jnp.int32, tall, 0) == lane
     devices = row_count * col_count
     spot_mine = place * col_count + cols_at
-    own = share.at[devices]
+    own = own_share.at[0]
     own[...] = jnp.sum(jnp.where(same & (here == 1), energy, 0.0), axis=0, keepdims=True)
 
     @pl.when(has_lower & jnp.logical_not(has_upper))
@@ -851,9 +875,7 @@
 
     lax.fori_loop(0, row_count, tell, 0)
     pltpu.make_async_copy(own, share.at[spot_mine], share_recv).start()
-    everyone = share.at[pl.ds(0, devices)]
-    pltpu.make_async_copy(everyone, everyone, share_recv).wait()
-    energy_ref[...] = jnp.sum(share[:devices], axis=0)[:, :terms]
+    pltpu.make_async_copy(share, share, share_recv).wait()
     others = share.at[pl.ds(0, devices - 1)]
     pltpu.make_async_copy(others, others, share_send).wait()
 
@@ -929,10 +951,10 @@
         functools.partial(window_kernel, row_count, col_count),
         out_shape=(
             jax.ShapeDtypeStruct((2, local_cols, chi, width), jnp.float32),
-            jax.ShapeDtypeStruct((1, terms), jnp.float32),
+            jax.ShapeDtypeStruct((row_count * col_count, 1, LANES), jnp.float32),
         ),
         in_specs=[vmem] + [stay] * 6 + [vmem] * 4,
-        out_specs=(stay, vmem),
+        out_specs=(stay, stay),
         scratch_shapes=[
             f32(2, local_cols, entries, LANES),
             f32(local_cols + 1, 2, entries, LANES),
@@ -947,20 +969,20 @@
             f32(D2**3, width),
             bf16(width, wide),
             bf16(width, width),
-            bf16(group, 2, width, LANES),
+            bf16(group, width, 2 * LANES),
             f32(width, width),
             bf16(group, D2 * width, 2 * width),
-            bf16(2 * LANES, width),
+            bf16(2 * LANES, 2 * width),
             f32(D2 * chi, wide),
             bf16(wide, pairs * wide),
             bf16(wide, pairs * wide),
             bf16(2, local_cols + 1, 2 * chi, wide),
-            bf16(2, local_cols + 1, 2, LANES, wide),
+            bf16(2, local_cols + 1, 3 * LANES, wide),
             f32(D2 * chi, LANES),
             f32(2, local_cols, pairs, chi, wide),
             f32(2, chi, width),
             f32(2, chi, width),
-            f32(row_count * col_count + 1, 1, LANES),
+            f32(1, 1, LANES),
             f32(1, terms, LANES),
             pltpu.SemaphoreType.REGULAR((2,)),
             dma((6,)),
@@ -987,9 +1009,53 @@
     )(*args[:7], *(index[None] for index in args[7:10]), args[10])
 
 
+def settle_kernel(
+    outs_ref, share_ref, top_ref, bottom_ref, energies_ref, held, shares, line, sem
+):
+    gather = pltpu.make_async_copy(share_ref, shares, sem.at[0, 0])
+    gather.start()
+    parts = [
+        (outs_ref.at[way, at], held.at[way, at], (top_ref, bottom_ref)[way].at[0, at])
+        for way in range(2)
+        for at in range(held.shape[1])
+    ]
+    for at, (source, middle, target) in enumerate(parts):
+        pltpu.make_async_copy(source, middle, sem.at[0, at + 1]).start()
+    gather.wait()
+    line[...] = jnp.sum(shares[...], axis=0)[:, : line.shape[1]]
+    put = pltpu.make_async_copy(line, energies_ref, sem.at[1, 0])
+    put.start()
+    for at, (source, middle, target) in enumerate(parts):
+        pltpu.make_async_copy(source, middle, sem.at[0, at + 1]).wait()
+        pltpu.make_async_copy(middle, target, sem.at[1, at + 1]).start()
+    for at, (source, middle, target) in enumerate(parts):
+        pltpu.make_async_copy(middle, target, sem.at[1, at + 1]).wait()
+    put.wait()
+
+
+def settle(outs, shares, terms):
+    stay = pl.BlockSpec(memory_space=pltpu.HBM)
+    half = jax.ShapeDtypeStruct((1,) + outs.shape[1:], outs.dtype)
+    count = outs.shape[0] * outs.shape[1] + 1
+    return pl.pallas_call(
+        settle_kernel,
+        out_shape=(half, half, jax.ShapeDtypeStruct((1, terms), shares.dtype)),
+        in_specs=[stay] * 2,
+        out_specs=(stay,) * 3,
+        scratch_shapes=[
+            pltpu.VMEM(outs.shape, outs.dtype),
+            pltpu.VMEM(shares.shape, shares.dtype),
+            pltpu.VMEM((1, terms), shares.dtype),
+            pltpu.SemaphoreType.DMA((2, count)),
+        ],
+        name="settle",
+    )(outs, shares)
+
+
 def shards(*args):
-    outs, energies = window(lax.axis_size("rows"), lax.axis_size("cols"), args)
-    return (outs[0][None], outs[1][None], energies[0])
+    outs, shares = window(lax.axis_size("rows"), lax.axis_size("cols"), args)
+    top, bottom, energies = settle(outs, shares, args[7].shape[0])
+    return (top, bottom, energies[0])
 
 
 def solution(mesh):

time: 70.7 us -> 68.8 us (0.973)
  local copies, waits for them, and re-layouts: 3.01 us -> 0 us
  Pallas kernels: 66.8 us -> 67.9 us
    slice x1 -> x0, local copies, waits for them, and re-layouts: 1.9 us -> none  [shards(): return (outs[0][None], outs[1][None], energies[0])]
    pallas_call x0 -> x1, Pallas kernels: none -> 1.89 us  [settle(): pl.pallas_call(settle_kernel, out_shape=(half, half, jax.ShapeDtypeStruct...]
    unnamed x3 -> x0, local copies, waits for them, and re-layouts: 1.1 us -> none
    pallas_call x1, Pallas kernels: 66.8 us -> 66 us  [window(): pl.pallas_call(functools.partial(window_kernel, row_count, col_count), ou...]
where the time goes in v4:
time: 68.8 us; the launch traced here: 68.6 us
  Pallas kernels  67.9 us (99%)
    pallas_call x1, Pallas kernels, window(): pl.pallas_call(functools.partial(window_kernel, row_count, col_count), ou...  66 us
    pallas_call x1, Pallas kernels, settle(): pl.pallas_call(settle_kernel, out_shape=(half, half, jax.ShapeDtypeStruct...  1.89 us

profile of v4, /device:TPU:0, one launch (start us, length us, event | category | flops | bytes accessed | tf_op | source)
XLA Modules:
  0.0 68.6 jit_solution(13223056123490118586)
XLA Ops:
  0.6 66.0 %window.1 = (f32[2,2,96,384]{3,2,1,0:T(8,128)}, f32[32,1,128]{2,1,0:T(1,128)}) custom-call(f32[1,2,32]{2,1,0:T(2,128)} %kets_ref.1, f32[2,1,2,96,384]{4,3,2,1,0:T(8,128)} %left_maps_ref.1, f32[2,1,2,96,384]{4,3,2,1,0:T(8,128)} %right_maps_ref.1, f32[2,96,384]{2,1,0:T(8,128)} %top_ref.1, f32[2,96,384]{2,1,0:T(8,128)} %bottom_ref.1, f32[1,96,384]{2,1,0:T(8,128)} %left_ref.1, ...), custom_call_target="tpu_custom_call" | custom-call | tf_op jit(solution)/shard_map/window/pallas_call | solution.py:950
  66.7 1.9 %settle.1 = (f32[1,2,96,384]{3,2,1,0:T(8,128)}, f32[1,2,96,384]{3,2,1,0:T(8,128)}, f32[1,16]{1,0:T(1,128)}) custom-call(f32[2,2,96,384]{3,2,1,0:T(8,128)} %get-tuple-element.8.outs_ref, f32[32,1,128]{2,1,0:T(1,128)} %get-tuple-element.9.share_ref), custom_call_target="tpu_custom_call" | custom-call | tf_op jit(solution)/shard_map/settle/pallas_call | solution.py:1040

commit v5 on v4

--- a/solution.py
+++ b/solution.py
@@ -587,11 +587,16 @@
                 far[1, at, rows, lanes] = turned
                 far[0, at, rows, lanes] = tall_block
 
-    def take_near(at):
-        for lanes, part, values, tall_block, turned in take_blocks(late, at):
-            rows = slice(part * chi, (part + 1) * chi)
-            near[0, at, rows, lanes] = turned[:chi]
-            near[1, at, rows, lanes] = values
+    def take_near(side, at):
+        blocks = unpack_lanes(load_tiles(env_ref.at[late], at, width), chi)
+        for d, block in enumerate(blocks):
+            lanes = slice(d * LANES, (d + 1) * LANES)
+            for part, values in enumerate(halves(block)):
+                rows = slice(part * chi, (part + 1) * chi)
+                if side == 0:
+                    values = dot_last(unit, jnp.concatenate([values, fill], axis=0))
+                    values = values.astype(jnp.bfloat16)[:chi]
+                near[rows, lanes] = values
 
     second = jnp.where(rank >= col_count // 2, 1, 0)
 
@@ -679,7 +684,7 @@
         lax.fori_loop(0, chi // chunk, through, 0)
 
     def close(side, at_column, pair):
-        both = near[true_side(side), at_column]
+        both = near[...]
         lanes = slice(pair * wide, (pair + 1) * wide)
         large = dot32(both, thi[:, lanes])
         opens[true_side(side), at_column - side, pair] = large[:chi] + (
@@ -729,8 +734,6 @@
         return unused
 
     lax.fori_loop(0, 2, phase, 0)
-    for at in range(1, local_cols + 1):
-        take_near(at)
 
     spot_row = lax.broadcasted_iota(jnp.int32, (terms, terms), 0)
     spot_lane = lax.broadcasted_iota(jnp.int32, (terms, terms), 1)
@@ -754,14 +757,23 @@
         opening = order == first_order(side)
         ending = order == local_cols - 1
 
+        fresh = (turn < local_cols) | (at_column == side * local_cols)
+
+        @pl.when(jnp.logical_not(absent) & fresh)
+        def _():
+            landed = env_ref.at[late, at_column]
+            pltpu.make_async_copy(landed, landed, env_recv.at[late, at_column]).wait()
+
+        for at in range(2):
+
+            @pl.when(jnp.logical_not(absent) & (true_side(side) == at))
+            def _():
+                take_near(at, at_column)
+
         @pl.when((order == 0) & jnp.logical_not(is_edge(side)))
         def _():
             pltpu.make_async_copy(hop_in.at[side], hop_in.at[side], hop_recv.at[side]).wait()
             put_environ(unpack_lanes(load_tiles(hop_in, side, width), chi))
-
-        @pl.when(jnp.logical_not(absent) & (at_column == 0))
-        def _():
-            take_near(0)
 
         @pl.when(jnp.logical_not(absent) & opening & is_edge(side))
         def _():
@@ -777,7 +789,9 @@
                 for q in range(PHYS):
                     close(side, at_column, p * PHYS + q)
 
-        @pl.when(jnp.logical_not(absent))
+        asked = jnp.where(side == 0, has_next, has_prev) | jnp.logical_not(ending)
+
+        @pl.when(jnp.logical_not(absent) & asked)
         def _():
             closed = opens[true_side(side), at_column - side, 0]
             for p in range(1, PHYS):
@@ -976,7 +990,7 @@
             f32(D2 * chi, wide),
             bf16(wide, pairs * wide),
             bf16(wide, pairs * wide),
-            bf16(2, local_cols + 1, 2 * chi, wide),
+            bf16(2 * chi, wide),
             bf16(2, local_cols + 1, 3 * LANES, wide),
             f32(D2 * chi, LANES),
             f32(2, local_cols, pairs, chi, wide),

time: 68.8 us -> 68.2 us (level)
  no operation moved by 1% of the time
where the time goes in v5:
time: 68.2 us; the launch traced here: 68 us
  Pallas kernels  67.3 us (99%)
    pallas_call x1, Pallas kernels, window(): pl.pallas_call(functools.partial(window_kernel, row_count, col_count), ou...  65.4 us
    pallas_call x1, Pallas kernels, settle(): pl.pallas_call(settle_kernel, out_shape=(half, half, jax.ShapeDtypeStruct...  1.89 us

profile of v5, /device:TPU:0, one launch (start us, length us, event | category | flops | bytes accessed | tf_op | source)
XLA Modules:
  0.0 68.0 jit_solution(7402536208616629853)
XLA Ops:
  0.6 65.4 %window.1 = (f32[2,2,96,384]{3,2,1,0:T(8,128)}, f32[32,1,128]{2,1,0:T(1,128)}) custom-call(f32[1,2,32]{2,1,0:T(2,128)} %kets_ref.1, f32[2,1,2,96,384]{4,3,2,1,0:T(8,128)} %left_maps_ref.1, f32[2,1,2,96,384]{4,3,2,1,0:T(8,128)} %right_maps_ref.1, f32[2,96,384]{2,1,0:T(8,128)} %top_ref.1, f32[2,96,384]{2,1,0:T(8,128)} %bottom_ref.1, f32[1,96,384]{2,1,0:T(8,128)} %left_ref.1, ...), custom_call_target="tpu_custom_call" | custom-call | tf_op jit(solution)/shard_map/window/pallas_call | solution.py:964
  66.1 1.9 %settle.1 = (f32[1,2,96,384]{3,2,1,0:T(8,128)}, f32[1,2,96,384]{3,2,1,0:T(8,128)}, f32[1,16]{1,0:T(1,128)}) custom-call(f32[2,2,96,384]{3,2,1,0:T(8,128)} %get-tuple-element.8.outs_ref, f32[32,1,128]{2,1,0:T(1,128)} %get-tuple-element.9.share_ref), custom_call_target="tpu_custom_call" | custom-call | tf_op jit(solution)/shard_map/settle/pallas_call | solution.py:1054

commit v6 on v5

--- a/solution.py
+++ b/solution.py
@@ -510,6 +510,10 @@
         def _():
             prepare(step, 0)
 
+        @pl.when(has_next & (column == edge_col))
+        def _():
+            side_copy(step, slot).start()
+
         send_row(
             xbuf.at[step],
             env_ref.at[way, spot_of(column)],
@@ -517,10 +521,6 @@
             env_recv.at[way, spot_of(column)],
             slot,
         )
-
-        @pl.when(has_next & (column == edge_col))
-        def _():
-            side_copy(step, slot).start()
 
         renewed = absorbed(step)
         put_right(renewed * known)

time: 68.2 us -> 68.3 us (level)
  no operation moved by 1% of the time
where the time goes in v6:
time: 68.3 us; the launch traced here: 68.1 us
  Pallas kernels  67.4 us (99%)
    pallas_call x1, Pallas kernels, window(): pl.pallas_call(functools.partial(window_kernel, row_count, col_count), ou...  65.5 us
    pallas_call x1, Pallas kernels, settle(): pl.pallas_call(settle_kernel, out_shape=(half, half, jax.ShapeDtypeStruct...  1.89 us

profile of v6, /device:TPU:0, one launch (start us, length us, event | category | flops | bytes accessed | tf_op | source)
XLA Modules:
  0.0 68.1 jit_solution(11936628186183283662)
XLA Ops:
  0.6 65.5 %window.1 = (f32[2,2,96,384]{3,2,1,0:T(8,128)}, f32[32,1,128]{2,1,0:T(1,128)}) custom-call(f32[1,2,32]{2,1,0:T(2,128)} %kets_ref.1, f32[2,1,2,96,384]{4,3,2,1,0:T(8,128)} %left_maps_ref.1, f32[2,1,2,96,384]{4,3,2,1,0:T(8,128)} %right_maps_ref.1, f32[2,96,384]{2,1,0:T(8,128)} %top_ref.1, f32[2,96,384]{2,1,0:T(8,128)} %bottom_ref.1, f32[1,96,384]{2,1,0:T(8,128)} %left_ref.1, ...), custom_call_target="tpu_custom_call" | custom-call | tf_op jit(solution)/shard_map/window/pallas_call | solution.py:964
  66.2 1.9 %settle.1 = (f32[1,2,96,384]{3,2,1,0:T(8,128)}, f32[1,2,96,384]{3,2,1,0:T(8,128)}, f32[1,16]{1,0:T(1,128)}) custom-call(f32[2,2,96,384]{3,2,1,0:T(8,128)} %get-tuple-element.8.outs_ref, f32[32,1,128]{2,1,0:T(1,128)} %get-tuple-element.9.share_ref), custom_call_target="tpu_custom_call" | custom-call | tf_op jit(solution)/shard_map/settle/pallas_call | solution.py:1054
